TPU v7x, 32 devices: a whole 2x2x4 slice. The times are simulated.
32 devices in a mesh: gx: 2 (over core), gy: 4 (over y, x), gz: 4 (over z).
Axes of the slice: x: 2, y: 2, z: 4, core: 2. Of those that a mesh axis runs over, the one named last changes fastest.
Arguments:
- sources: float32 [1, 32, 64, 512], P(None, 'gx', 'gy', 'gz'), may hold values from -6 to 6
- stiffness: float32 [32, 64, 512], P('gx', 'gy', 'gz'), may hold values from 0.5 to 2
- coarse_inverse: float32 [256, 256], P(('gx', 'gy', 'gz')), may hold values from -6 to 6
Outputs:
- pressure: float32 [1, 32, 64, 512], P(None, 'gx', 'gy', 'gz')
All inputs are finite; a program needn't handle non-finite values.
Results may differ from a plain program's by a relative error of at most 0.0001.
Values sent between devices are 32-bit elements; how exact they have to be, the bound alone decides.
No kernel may reach another device: no remote copies, remote signals or barrier semaphores. Data moves between devices by JAX's collectives and lax.ppermute only.
A program may use at most 64 MiB of HBM per device.

v0:
```python
import functools
import math

import jax
import jax.numpy as jnp
from jax import lax
from jax.experimental import pallas as pl
from jax.experimental.pallas import tpu as pltpu
from jax.sharding import PartitionSpec as P


damping = 0.8
K = damping / 6.0
AXES = ("gx", "gy", "gz")
HALO = 8
F32 = jnp.float32


def swap(values, axis, first):
    count = lax.axis_size(axis)
    partner = list(range(count))
    for i in range(first, count - 1, 2):
        partner[i], partner[i + 1] = i + 1, i
    return lax.ppermute(values, axis, list(enumerate(partner)))


def ring(values, axis, step):
    count = lax.axis_size(axis)
    return lax.ppermute(values, axis, [(i, (i + step) % count) for i in range(count)])


def iota(shape, dim):
    return lax.broadcasted_iota(jnp.int32, shape, dim)


def roll(values, amount):
    size = values.shape[-1]
    if isinstance(amount, int):
        amount = amount % size
        if amount == 0:
            return values
    return pltpu.roll(values, amount, values.ndim - 1)


def z_sum(main, side, step):
    lane = iota(main.shape, main.ndim - 1)
    size = main.shape[-1]
    main_up, side_up = roll(main, -step), roll(side, -step)
    main_dn, side_dn = roll(main, step), roll(side, step)
    last = lane >= size - step
    first = lane < step
    main_sum = jnp.where(last, side_up, main_up) + jnp.where(first, side_dn, main_dn)
    side_sum = jnp.where(last, main_up, side_up) + jnp.where(first, main_dn, side_dn)
    return main_sum, side_sum


def xy_sum(ref, x, row, rows):
    total = ref[x - 1, pl.ds(row, rows), :] + ref[x + 1, pl.ds(row, rows), :]
    return total + ref[x, pl.ds(row - 1, rows), :] + ref[x, pl.ds(row + 1, rows), :]


def neighbours(main_ref, side_ref, x, row, rows, step):
    main = main_ref[x, pl.ds(row, rows), :]
    side = side_ref[x, pl.ds(row, rows), :]
    main_z, side_z = z_sum(main, side, step)
    return main, side, xy_sum(main_ref, x, row, rows) + main_z, xy_sum(side_ref, x, row, rows) + side_z


def global_neighbours(ref, x, row, rows, step):
    main = ref[x, pl.ds(row, rows), :]
    lane = iota(main.shape, 1)
    size = main.shape[-1]
    up = jnp.where(lane >= size - step, 0.0, roll(main, -step))
    dn = jnp.where(lane < step, 0.0, roll(main, step))
    return main, xy_sum(ref, x, row, rows) + up + dn


def lane_pairs(values, step):
    lane = iota(values.shape, values.ndim - 1)
    return values + jnp.where((lane // step) % 2 == 0, roll(values, -step), roll(values, step))


def inverse(weights):
    return jnp.where(weights > 0.0, 1.0 / jnp.where(weights > 0.0, weights, 1.0), 0.0)


def tiled(value):
    return [value[:, t * 128 : (t + 1) * 128] for t in range(value.shape[1] // 128)]


def joined(parts):
    return parts[0] if len(parts) == 1 else jnp.concatenate(parts, axis=1)


def row_pairs(ref, rows):
    return joined([ref[t, pl.ds(0, rows // 2, stride=2), :] + ref[t, pl.ds(1, rows // 2, stride=2), :] for t in range(ref.shape[0])])


def each(count, body, width=1):
    while count % width:
        width -= 1
    if count == width:
        for i in range(count):
            body(i)
        return

    def step(i, carry):
        for j in range(width):
            body(i * width + j)
        return carry

    lax.fori_loop(0, count // width, step, 0)


def pair_places(axis, count, own, tall):
    index = lax.axis_index(axis)
    odd = index % 2
    first = dict(place=jnp.where(odd == 0, own + tall, 0), high=odd == 0, valid=jnp.where(odd == 0, index + 1, index - 1) < count)
    other = jnp.where(odd == 0, index - 1, index + 1)
    second = dict(place=jnp.where(odd == 0, 0, own + tall), high=odd == 1, valid=(other >= 0) & (other < count))
    return index, odd, (first, second)


def x_frame(count, tall):
    index = lax.axis_index("gx")
    odd = index % 2
    if count == 1:
        return index, 0, ()
    own = HALO * odd if count == 2 else HALO
    _, _, (first, second) = pair_places("gx", count, own, tall)
    if count == 2:
        first["source"] = jnp.where(odd == 0, 0, tall - HALO)
        return index, own, (first,)
    first["source"] = second["source"] = 0
    return index, own, (first, second)


def y_ends(count, wide):
    index = lax.axis_index("gy")
    return (dict(valid=index > 0, place=0, high=0), dict(valid=index < count - 1, place=wide + HALO, high=1))


def frame_extent(count, tall):
    return tall + (0 if count == 1 else HALO if count == 2 else 2 * HALO)


def keep(valid, values):
    return jnp.where(valid, values, jnp.zeros_like(values))


def y_pack_kernel(mesh_shape, *refs):
    n_gx, _, _ = mesh_shape
    n_in = 3 * (1 + min(n_gx - 1, 2))
    own_refs, part_refs, outs = refs[:3], refs[3:n_in], refs[n_in:]
    tall, wide = own_refs[0].shape[0], own_refs[0].shape[1]
    extent = frame_extent(n_gx, tall)
    tiles = own_refs[2].shape[1] // 128
    _, own, parts = x_frame(n_gx, tall)
    for out, start in zip(outs, (wide - HALO, 0)):
        rows = pl.ds(start, HALO)
        for a in range(2):
            out[pl.ds(a * extent + own, tall)] = own_refs[a][:, rows, :]
            for part, ref in zip(parts, (part_refs[a : a + 1], part_refs[3 + a : 4 + a])):
                out[pl.ds(a * extent + part["place"], HALO)] = keep(part["valid"], ref[0][pl.ds(part["source"], HALO), rows, :])
        base = 2 * extent
        for side in (0, 2):
            for t in range(tiles):
                out[base + side * tiles + t] = jnp.zeros((HALO, 128), F32)
        for t in range(tiles):
            out[base + tiles + t] = own_refs[2][:, t * 128 : (t + 1) * 128]
            for part, ref in zip(parts, (part_refs[2:3], part_refs[5:6])):
                side = jnp.where(part["high"], 2, 0)
                out[base + side * tiles + t] = keep(part["valid"], ref[0][:, t * 128 : (t + 1) * 128])


def z_pack_kernel(mesh_shape, *refs):
    n_gx, n_gy, _ = mesh_shape
    n_in = 3 * (1 + min(n_gx - 1, 2))
    own_refs, part_refs = refs[:3], refs[3:n_in]
    y_refs = refs[n_in : n_in + 2]
    frames = refs[n_in + 2 : n_in + 4]
    rows_ref, z_outs = refs[n_in + 4], refs[n_in + 5 :]
    tall, wide = own_refs[0].shape[0], own_refs[0].shape[1]
    extent = frame_extent(n_gx, tall)
    tiles = own_refs[2].shape[1] // 128
    _, own, parts = x_frame(n_gx, tall)
    y_parts = y_ends(n_gy, wide)
    for a in range(2):
        frames[a][pl.ds(own, tall), HALO : HALO + wide, :] = own_refs[a][...]
        for part, ref in zip(parts, (part_refs[a : a + 1], part_refs[3 + a : 4 + a])):
            frames[a][pl.ds(part["place"], HALO), HALO : HALO + wide, :] = keep(part["valid"], ref[0][pl.ds(part["source"], HALO)])
        for part, ref in zip(y_parts, y_refs):
            rows = pl.ds(part["place"], HALO)
            frames[a][:, rows, :] = keep(part["valid"], ref[a * extent : (a + 1) * extent])
    for t in range(tiles):
        for side in (0, 2):
            rows_ref[(side * 3 + 1) * tiles + t] = jnp.zeros((HALO, 128), F32)
        rows_ref[4 * tiles + t] = own_refs[2][:, t * 128 : (t + 1) * 128]
        for part, ref in zip(parts, (part_refs[2:3], part_refs[5:6])):
            side = jnp.where(part["high"], 2, 0)
            rows_ref[(side * 3 + 1) * tiles + t] = keep(part["valid"], ref[0][:, t * 128 : (t + 1) * 128])
        for x_side in range(3):
            for part, ref in zip(y_parts, y_refs):
                side = 2 * part["high"]
                rows_ref[(x_side * 3 + side) * tiles + t] = keep(part["valid"], ref[2 * extent + x_side * tiles + t])
    groups = extent // HALO
    for out, tail in zip(z_outs, (1, 0)):

        def put(group, packed):
            out[group] = packed

        pack_z(frames, put, tail)
        row = (HALO - 1) * tail
        for s in range((tiles + 1) // 2):
            out[groups + s] = jnp.zeros((4 * HALO, 128), F32)
        for t in range(tiles):
            for m in range(9):
                out[groups + t // 2, 16 * (t % 2) + m : 16 * (t % 2) + m + 1, :] = rows_ref[m * tiles + t, row : row + 1, :]


def z_ends(count):
    index = lax.axis_index("gz")
    return (dict(valid=index > 0, lane=120, row=-1), dict(valid=index < count - 1, lane=0, row=HALO))


def pack_z(frames, out, tail):
    rows = frames[0].shape[1]
    slot = iota((rows, 128), 1) // HALO
    for group in range(frames[0].shape[0] // HALO):
        packed = jnp.zeros((rows, 128), F32)
        for i in range(HALO):
            for a in range(2):
                piece = roll(frames[a][group * HALO + i], 8 * (tail + 2 * i + a))
                packed = jnp.where(slot == 2 * i + a, piece, packed)
        out(group, packed)


def face_kernel(*refs):
    b, w, matrix, *outs = refs
    outs, y_outs, both, copies = outs[:2], outs[2:4], outs[4], outs[5:]
    tall, wide = b.shape[0], b.shape[1]
    tiles = matrix.shape[1] // 128
    strips = (tiles + 7) // 8
    per = wide // 8
    for out, tail in zip(outs, (1, 0)):

        def put(group, packed):
            for r in range(per):
                out[group * per + r] = packed[8 * r : 8 * r + 8]

        pack_z((b, w), put, tail)
        at = tall // HALO * per
        line = matrix[HALO - 1 : HALO, :] if tail else matrix[0:1, :]
        for strip in range(strips):
            out[at + strip] = jnp.zeros((8, 128), F32)
        for t in range(tiles):
            out[at + t // 8, t % 8 : t % 8 + 1, :] = line[:, t * 128 : (t + 1) * 128]
    for out, row in zip(y_outs, (wide - HALO, 0)):
        for a, ref in enumerate((b, w)):
            out[a * tall : (a + 1) * tall] = ref[:, row : row + HALO, :]
        for t in range(tiles):
            out[2 * tall + t] = matrix[:, t * 128 : (t + 1) * 128]
    at = 0
    for ref in (b, w):
        for r in range(per):
            both[at : at + tall] = ref[:, 8 * r : 8 * r + 8, :]
            at += tall
    for t in range(tiles):
        both[at + t] = matrix[:, t * 128 : (t + 1) * 128]
    for ref, copy in zip((b, w, matrix), copies):
        copy[...] = ref[...]


def y_edge_kernel(groups, per, *refs):
    z_refs, outs, both = refs[:2], refs[2:4], refs[4]
    size = z_refs[0].shape[0]
    strips = size - groups * per
    for out, r in zip(outs, (per - 1, 0)):
        for k, ref in enumerate(z_refs):
            at = k * (groups + strips)
            for group in range(groups):
                out[at + group] = ref[group * per + r]
            out[at + groups : at + groups + strips] = ref[groups * per : size]
    for k, ref in enumerate(z_refs):
        both[k * size : (k + 1) * size] = ref[...]


def frame_kernel(mesh_shape, *refs):
    n_gx, n_gy, _ = mesh_shape
    own_refs, other, z_refs, z_other = refs[:3], refs[3], refs[4:6], refs[6]
    y_refs, y_others, edge_refs, edge_others = refs[7:9], refs[9:11], refs[11:13], refs[13:15]
    frames, rows_ref, z_outs = refs[15:17], refs[17], refs[18:]
    tall, wide = own_refs[0].shape[0], own_refs[0].shape[1]
    extent = frame_extent(n_gx, tall)
    tiles = own_refs[2].shape[1] // 128
    strips, groups, per = (tiles + 7) // 8, tall // HALO, wide // 8
    _, own, parts = x_frame(n_gx, tall)
    place, source = parts[0]["place"], parts[0]["source"]
    y_parts = y_ends(n_gy, wide)
    far = jnp.where(parts[0]["high"], 2, 0)
    y_rows = [pl.ds(p["place"], HALO) for p in y_parts]
    y_side = [2 * p["high"] for p in y_parts]
    for a in range(2):
        frames[a][pl.ds(own, tall), HALO : HALO + wide, :] = own_refs[a][...]
        for r in range(per):
            rows = slice(HALO + 8 * r, HALO + 8 * r + 8)
            frames[a][pl.ds(place, HALO), rows, :] = other[pl.ds((a * per + r) * tall + source, HALO)]
        for part, rows, ref, ref_other in zip(y_parts, y_rows, y_refs, y_others):
            frames[a][pl.ds(own, tall), rows, :] = keep(part["valid"], ref[a * tall : (a + 1) * tall])
            frames[a][pl.ds(place, HALO), rows, :] = keep(part["valid"], ref_other[pl.ds(a * tall + source, HALO)])
    zero = jnp.zeros((HALO, 128), F32)
    for t in range(tiles):
        for side in range(3):
            rows_ref[((2 - far) * 3 + side) * tiles + t] = zero
        rows_ref[4 * tiles + t] = own_refs[2][:, t * 128 : (t + 1) * 128]
        rows_ref[(far * 3 + 1) * tiles + t] = other[2 * per * tall + t]
        for part, side, ref, ref_other in zip(y_parts, y_side, y_refs, y_others):
            rows_ref[(3 + side) * tiles + t] = keep(part["valid"], ref[2 * tall + t])
            rows_ref[(far * 3 + side) * tiles + t] = keep(part["valid"], ref_other[2 * tall + t])
    for k, (out, ref) in enumerate(zip(z_outs, z_refs)):
        base = k * (groups * per + strips)
        y_base = k * (groups + strips)
        total = extent // HALO
        for s in range((tiles + 1) // 2):
            out[total + s] = jnp.zeros((4 * HALO, 128), F32)
        for g in range(groups):
            for r in range(per):
                out[own // HALO + g, HALO + 8 * r : HALO + 8 * r + 8, :] = ref[g * per + r]
            for part, rows, y_ref in zip(y_parts, y_rows, edge_refs):
                out[own // HALO + g, rows, :] = keep(part["valid"], y_ref[y_base + g])
        for r in range(per):
            out[place // HALO, HALO + 8 * r : HALO + 8 * r + 8, :] = z_other[base + source // HALO * per + r]
        for part, rows, y_ref in zip(y_parts, y_rows, edge_others):
            out[place // HALO, rows, :] = keep(part["valid"], y_ref[y_base + source // HALO])
        for strip in range(strips):
            for x_side in range(3):
                if x_side == 1:
                    middle = ref[groups * per + strip]
                    edges = [keep(p["valid"], r[y_base + groups + strip]) for p, r in zip(y_parts, edge_refs)]
                else:
                    here = far == x_side
                    middle = keep(here, z_other[base + groups * per + strip])
                    edges = [keep(p["valid"] & here, r[y_base + groups + strip]) for p, r in zip(y_parts, edge_others)]
                low, high = edges
                for j in range(min(8, tiles - 8 * strip)):
                    t = 8 * strip + j
                    for side, values in enumerate((low, middle, high)):
                        m = 16 * (t % 2) + x_side * 3 + side
                        out[total + t // 2, m : m + 1, :] = values[j : j + 1]


def down_kernel(mesh_shape, *refs):
    n_gx, _, n_gz = mesh_shape
    fb, fw, za, zb = refs[:4]
    send, v0w, w0w, v0h, w0h, g0, v1m, v1s, w1m, w1s, g1m, g1s = refs[4:16]
    gm, gs, vm, vs, ws, tm, ts, um, us, small = refs[16:]
    extent, rows = fb.shape[0], fb.shape[1]
    tall = g0.shape[0]
    wide = g0.shape[1]
    half, half_rows = extent // 2, rows // 2
    _, own, _ = x_frame(n_gx, tall)
    groups = extent // HALO
    zero = jnp.zeros((8, 128), F32)

    def clear(ref, count, depth):
        for x in (0, count + 1):
            for r in range(0, depth + 16, 8):
                ref[x, r : r + 8, :] = zero
        for x in range(1, count + 1):
            ref[x, 0:8, :] = zero
            ref[x, depth + 8 : depth + 16, :] = zero

    for ref in (gm, gs, vm, vs):
        clear(ref, extent, rows)
    for ref in (v1m, v1s, g1m, g1s, w1m, w1s):
        clear(ref, half, half_rows)

    lane = iota((rows, 128), 1)
    ends = z_ends(n_gz)
    masks = [((lane >= e["lane"]) & (lane < e["lane"] + HALO)).astype(F32) * e["valid"].astype(F32) for e in ends]

    def load(group):
        for i in range(HALO):
            x = group * HALO + i
            sides = []
            for a in range(2):
                total = None
                for ref, mask, end in zip((za, zb), masks, ends):
                    piece = roll(ref[group], end["lane"] - 16 * i - 8 * a) * mask
                    total = piece if total is None else total + piece
                sides.append(total)
            ws[x] = sides[1]
            gm[x + 1, 8 : 8 + rows, :] = K * fb[x] * inverse(fw[x])
            gs[x + 1, 8 : 8 + rows, :] = K * sides[0] * inverse(sides[1])

    each(groups, load, 4)

    def second(x):
        main, side, main_n, side_n = neighbours(gm, gs, x + 1, 8, rows, 1)
        vm[x + 1, 8 : 8 + rows, :] = 1.2 * main + jnp.where(fw[x] > 0.0, K * main_n, 0.0)
        vs[x + 1, 8 : 8 + rows, :] = 1.2 * side + jnp.where(ws[x] > 0.0, K * side_n, 0.0)

    each(extent, second, 8)

    def residual(x2):
        totals = None
        for j in range(2):
            x = 2 * x2 + j
            main, side, main_n, side_n = neighbours(vm, vs, x + 1, 8, rows, 1)
            w_main, w_side = fw[x], ws[x]
            r_main = w_main * ((1.0 / K) * gm[x + 1, 8 : 8 + rows, :] - 6.0 * main + main_n)
            r_side = w_side * ((1.0 / K) * gs[x + 1, 8 : 8 + rows, :] - 6.0 * side + side_n)
            values = (r_main, r_side, w_main, w_side)
            totals = values if j == 0 else tuple(a + b for a, b in zip(totals, values))
        for ref, value in zip((tm, ts, um, us), totals):
            ref[x2] = value

        def pairs(ref):
            return lane_pairs(ref[x2, pl.ds(0, half_rows, stride=2), :] + ref[x2, pl.ds(1, half_rows, stride=2), :], 1)

        for t_ref, u_ref, w_out, g_out in ((tm, um, w1m, g1m), (ts, us, w1s, g1s)):
            weights = 0.0625 * pairs(u_ref)
            w_out[x2 + 1, 8 : 8 + half_rows, :] = weights
            g_out[x2 + 1, 8 : 8 + half_rows, :] = (0.125 * K) * pairs(t_ref) * inverse(weights)

    each(half, residual, 4)

    def second_1(x):
        main, side, main_n, side_n = neighbours(g1m, g1s, x + 1, 8, half_rows, 2)
        v1m[x + 1, 8 : 8 + half_rows, :] = 1.2 * main + jnp.where(w1m[x + 1, 8 : 8 + half_rows, :] > 0.0, K * main_n, 0.0)
        v1s[x + 1, 8 : 8 + half_rows, :] = 1.2 * side + jnp.where(w1s[x + 1, 8 : 8 + half_rows, :] > 0.0, K * side_n, 0.0)

    each(half, second_1, 16)

    base = own // 2
    first_row = 8 + HALO // 2
    quarter, quarter_rows = tall // 4, wide // 4
    for x2 in range(quarter):
        total_r = total_w = None
        for j in range(2):
            x = base + 2 * x2 + j + 1
            main, _, main_n, _ = neighbours(v1m, v1s, x, first_row, wide // 2, 2)
            weights = w1m[x, pl.ds(first_row, wide // 2), :]
            res = weights * ((1.0 / K) * g1m[x, pl.ds(first_row, wide // 2), :] - 6.0 * main + main_n)
            total_r = res if j == 0 else total_r + res
            total_w = weights if j == 0 else total_w + weights
        small[0, x2] = total_r
        small[1, x2] = total_w
    q = []
    for a, factor in ((0, 0.125), (1, 0.0625)):
        for x2 in range(quarter):
            ref = small.at[a, x2]
            both = ref[pl.ds(0, quarter_rows, stride=2), :] + ref[pl.ds(1, quarter_rows, stride=2), :]
            q.append(factor * lane_pairs(both, 2))
    stacked = jnp.concatenate([jnp.concatenate(q[:quarter], axis=0), jnp.concatenate(q[quarter:], axis=0)], axis=0)
    src, dst = iota((128, 128), 0), iota((128, 128), 1)
    pick = (src == 4 * (dst % 32)).astype(F32)
    compact = jnp.dot(stacked, pick, precision=lax.Precision.HIGHEST, preferred_element_type=F32)
    block = iota((quarter_rows, 128), 1) // 32
    gz = lax.axis_index("gz")
    out = []
    for a in range(2):
        packed = jnp.zeros((quarter_rows, 128), F32)
        for x2 in range(quarter):
            r = (a * quarter + x2) * quarter_rows
            packed = jnp.where(block == lax.rem(gz + x2, 4), compact[r : r + quarter_rows], packed)
        out.append(packed)
    message = jnp.concatenate(out, axis=0)

    def copy(d):
        send[d] = message

    each(send.shape[0], copy, 8)

    for i in range(tall + 2):
        v0w[i] = vm[own + i, 8 : 8 + rows, :]
        x = own + (i - 1)
        inside = (x >= 0) & (x < extent)
        w0w[i] = keep(inside, fw[jnp.clip(x, 0, extent - 1)])
    for i in range(tall):
        v0h[i] = vs[own + i + 1, 8 + HALO : 8 + HALO + wide, :]
        w0h[i] = ws[own + i, HALO : HALO + wide, :]
        g0[i] = gm[own + i + 1, 8 + HALO : 8 + HALO + wide, :]


def up_kernel(mesh_shape, *refs):
    n_gx, n_gy, n_gz = mesh_shape
    recv, rows_ref, za, zb, v0w, w0w, v0h, w0h, g0, v1m, v1s, w1m, w1s, g1m, g1s, out = refs[:16]
    g2, w2, v2, y2, e2, p2, t3, u3, g3, w3, v3, y3, p3, b4, _, y1m, y1s, e1m, e1s, f1m, f1s, y0m, y0s = refs[16:]
    tall, wide = out.shape[0], out.shape[1]
    size_x, size_z = w2.shape[0], w2.shape[2]
    size_y = w2.shape[1]
    ix, own, _ = x_frame(n_gx, tall)
    iy, iz = lax.axis_index("gy"), lax.axis_index("gz")
    quarter, quarter_rows = tall // 4, wide // 4
    extent = frame_extent(n_gx, tall)
    half, half_rows = v1m.shape[0] - 2, v1m.shape[1] - 16

    def clear(ref):
        count, depth, size = ref.shape
        zero = jnp.zeros((8, size), F32)
        for x in range(count):
            ref[x, 0:8, :] = zero
            ref[x, depth - 8 : depth, :] = zero
        for x in (0, count - 1):
            ref[x] = jnp.zeros((depth, size), F32)

    for ref in (g2, v2, y2, g3, v3, y3):
        clear(ref)
    e2[...] = jnp.zeros(e2.shape, F32)
    p3[...] = jnp.zeros(p3.shape, F32)

    lane = iota((quarter_rows, 128), 1)
    block = lane // 32
    for gx in range(n_gx):
        for gy in range(n_gy):
            for x in range(quarter):
                tiles_b, tiles_w = [], []
                for tile in range(size_z // 128):
                    picked = [jnp.zeros((quarter_rows, 128), F32)] * 2
                    for j in range(4):
                        gz = tile * 4 + j
                        d = (gx * n_gy + gy) * n_gz + gz
                        mask = block == (gz + x) % 4
                        for a in range(2):
                            piece = recv[d, a * quarter_rows : (a + 1) * quarter_rows, :]
                            picked[a] = jnp.where(mask, piece, picked[a])
                    tiles_b.append(roll(picked[0], -32 * x))
                    tiles_w.append(roll(picked[1], -32 * x))
                weights = joined(tiles_w)
                w2[gx * quarter + x, gy * quarter_rows : (gy + 1) * quarter_rows, :] = weights
                g2[gx * quarter + x + 1, 8 + gy * quarter_rows : 8 + (gy + 1) * quarter_rows, :] = K * joined(tiles_b) / weights

    def smooth(g, v, x, rows, step):
        main, near = global_neighbours(g, x + 1, 8, rows, step)
        v[x + 1, 8 : 8 + rows, :] = 1.2 * main + K * near

    def resid(g, v, w, x, rows, step):
        main, near = global_neighbours(v, x + 1, 8, rows, step)
        return w[x] * ((1.0 / K) * g[x + 1, 8 : 8 + rows, :] - 6.0 * main + near)

    each(size_x, lambda x: smooth(g2, v2, x, size_y, 1), 8)
    rows3, x3 = size_y // 2, size_x // 2

    def restrict_2(x):
        for t, part in enumerate(tiled(resid(g2, v2, w2, 2 * x, size_y, 1) + resid(g2, v2, w2, 2 * x + 1, size_y, 1))):
            t3[t] = part
        for t, part in enumerate(tiled(w2[2 * x] + w2[2 * x + 1])):
            u3[t] = part
        pairs = lambda ref: lane_pairs(row_pairs(ref, size_y), 1)
        weights = 0.0625 * pairs(u3)
        w3[x] = weights
        g3[x + 1, 8 : 8 + rows3, :] = (0.125 * K) * pairs(t3) / weights

    each(x3, restrict_2, 4)
    each(x3, lambda x: smooth(g3, v3, x, rows3, 2), 8)
    rows4, x4 = rows3 // 2, x3 // 2

    def restrict_3(x):
        for t, part in enumerate(tiled(resid(g3, v3, w3, 2 * x, rows3, 2) + resid(g3, v3, w3, 2 * x + 1, rows3, 2))):
            t3[t, 0:rows3, :] = part
        b4[x] = 0.125 * lane_pairs(row_pairs(t3, rows3), 2)

    each(x4, restrict_3, 4)

    tiles = rows_ref.shape[0] // 9
    coarse_z = size_z // 4
    per = 128 // coarse_z
    src, dst = iota((size_z, 128), 0), iota((size_z, 128), 1)
    pick = (src == 4 * (dst % coarse_z)).astype(F32)
    values = b4[0] if x4 == 1 else jnp.concatenate([b4[x] for x in range(x4)], axis=0)
    compact = jnp.dot(values, pick, precision=lax.Precision.HIGHEST, preferred_element_type=F32)
    place = iota((x4 * rows4, 128), 0) % per == iota((x4 * rows4, 128), 1) // coarse_z
    compact = jnp.where(place, compact, 0.0)
    vectors = [jnp.sum(compact[t * per : (t + 1) * per], axis=0, keepdims=True) for t in range(tiles)]
    ends = z_ends(n_gz)
    groups = extent // HALO
    fine = iota((HALO, size_z), 1) // 4
    fine_row = fine == iz * HALO + iota((HALO, size_z), 0)
    edge_row = iota((16, 128), 0)
    first_total = [None, None]
    for k, ref in enumerate((za, zb)):
        total = None
        for t in range(tiles):
            piece = ref[groups + t // 2, 16 * (t % 2) : 16 * (t % 2) + 16, :] * vectors[t]
            total = piece if total is None else total + piece
        first_total[k] = jnp.sum(total, axis=1, keepdims=True) * ends[k]["valid"].astype(F32)
    z_lane = iota((16, size_z), 1) // 4
    spread = None
    for k in range(2):
        piece = jnp.where(z_lane == iz * HALO + ends[k]["row"], first_total[k], 0.0)
        spread = piece if spread is None else spread + piece
    for m in range(9):
        total = None
        for t in range(tiles):
            piece = rows_ref[m * tiles + t] * vectors[t]
            total = piece if total is None else total + piece
        values = jnp.sum(total, axis=1, keepdims=True)
        line = jnp.sum(jnp.where(fine_row, values, 0.0), axis=0, keepdims=True) + spread[m : m + 1, :]
        row = 8 + 2 * (iy + (m % 3 - 1))
        for t, part in enumerate(tiled(line)):
            p3[ix + m // 3, t, pl.ds(row, 1), :] = part
            p3[ix + m // 3, t, pl.ds(row + 1, 1), :] = part

    def lift(y, v, w, p, x, px, rows, row):
        coarse = joined([p[px, t, row : row + rows, :] for t in range(p.shape[1])])
        y[x + 1, 8 : 8 + rows, :] = v[x + 1, 8 : 8 + rows, :] + w[x] * coarse

    def relax(y, g, w, x, rows, step):
        main, near = global_neighbours(y, x + 1, 8, rows, step)
        return (0.2 * main + g[x + 1, 8 : 8 + rows, :] + K * near) / w[x]

    each(x3, lambda x: lift(y3, v3, w3, p3, x, x // 2 + 1, rows3, 8), 8)

    def up_3(x):
        for t, e3 in enumerate(tiled(relax(y3, g3, w3, x, rows3, 2))):
            p2[x, t, pl.ds(0, rows3, stride=2), :] = e3
            p2[x, t, pl.ds(1, rows3, stride=2), :] = e3

    each(x3, up_3, 4)
    each(size_x, lambda x: lift(y2, v2, w2, p2, x, x // 2, size_y, 0), 8)

    def up_2(x):
        for t, part in enumerate(tiled(relax(y2, g2, w2, x, size_y, 1))):
            e2[x + 2, t, 8 : 8 + size_y, :] = part

    each(size_x, up_2, 8)

    src, dst = iota((size_z, 256), 0), iota((size_z, 256), 1)
    start = iz * 32
    cell = jnp.where(dst < 128, dst // 4, jnp.where(dst < 192, 32 + (dst - 128) // 4, -1 - (255 - dst) // 4))
    widen = (src == start + cell).astype(F32)
    n2 = extent // 4
    x_start = ix * quarter - own // 4
    y_start = 8 + iy * quarter_rows - HALO // 4
    spread = None
    for t in range(size_z // 128):
        stacked = jnp.concatenate([e2[x_start + 2 + i, t, pl.ds(y_start, 8), :] for i in range(n2)], axis=0)
        part = jnp.dot(stacked, widen[t * 128 : (t + 1) * 128], precision=lax.Precision.HIGHEST, preferred_element_type=F32)
        spread = part if spread is None else spread + part
    for i in range(n2):
        for ref, part in ((e1m, spread[i * 8 : i * 8 + 8, :128]), (e1s, spread[i * 8 : i * 8 + 8, 128:])):
            ref[i, pl.ds(0, 8, stride=2), :] = part
            ref[i, pl.ds(1, 8, stride=2), :] = part

    clear(y1m)
    clear(y1s)
    inner = slice(8, 8 + half_rows)
    for x in range(half):
        y1m[x + 1, inner, :] = v1m[x + 1, inner, :] + w1m[x + 1, inner, :] * e1m[x // 2]
        y1s[x + 1, inner, :] = v1s[x + 1, inner, :] + w1s[x + 1, inner, :] * e1s[x // 2]

    def up_1(x):
        main, side, main_n, side_n = neighbours(y1m, y1s, x + 1, 8, half_rows, 2)
        for f, y, near, g, w in ((f1m, main, main_n, g1m, w1m), (f1s, side, side_n, g1s, w1s)):
            e1 = (0.2 * y + g[x + 1, inner, :] + K * near) * inverse(w[x + 1, inner, :])
            f[x, pl.ds(0, half_rows, stride=2), :] = e1
            f[x, pl.ds(1, half_rows, stride=2), :] = e1

    each(half, up_1, 12)
    base = own // 2
    for i in range(tall + 2):
        parent = jnp.clip(base + (i + 1) // 2 - 1, 0, half - 1)
        y0m[i] = v0w[i] + w0w[i] * f1m[parent]
        if 0 < i <= tall:
            y0s[i - 1] = v0h[i - 1] + w0h[i - 1] * f1s[parent, HALO : HALO + wide, :]

    def up_0(i):
        main = y0m[i + 1, pl.ds(HALO, wide), :]
        main_z, _ = z_sum(main, y0s[i], 1)
        near = xy_sum(y0m, i + 1, HALO, wide) + main_z
        out[i] = (0.2 * main + g0[i] + K * near) / w0w[i + 1, HALO : HALO + wide, :]

    each(tall, up_0, 16)


def size_of(shape):
    return 4 * math.prod(shape)


def call(kernel, outs, scratch=(), resident=True, fetch=False):
    limit = 8 * 2**20 + sum(map(size_of, scratch)) + sum(size_of(s) for s in outs if size_of(s) > 2**20)
    run = pl.pallas_call(
        kernel,
        out_shape=[(pltpu.VMEM if resident and size_of(s) <= 2**20 else jax.ShapeDtypeStruct)(s, F32) for s in outs],
        scratch_shapes=[pltpu.VMEM(s, F32) for s in scratch],
        compiler_params=pltpu.CompilerParams(vmem_limit_bytes=min(limit, 56 * 2**20)),
    )

    def place(value):
        small = size_of(value.shape) <= 2**20 and not fetch
        return pltpu.with_memory_space_constraint(value, pltpu.VMEM if small else pltpu.HBM)

    return lambda *values: run(*map(place, values))


def plain_halo(mesh_shape, own, frames):
    n_gx = mesh_shape[0]
    tall = own[0].shape[0]
    extent, tiles = frames[0][0], own[2].shape[1] // 128
    parts = ()
    if n_gx > 1:
        odd = lax.axis_index("gx") % 2
        for first in range(2):
            start = jnp.where(odd == first, tall - HALO, 0)
            faces = [lax.dynamic_slice_in_dim(a, start, HALO, 0) for a in own[:2]] + [own[2]]
            parts += tuple(swap(a, "gx", first) for a in faces)
    slab = (2 * extent + 3 * tiles, HALO, 128)
    y_slabs = call(functools.partial(y_pack_kernel, mesh_shape), [slab, slab])(*own, *parts)
    y_parts = [ring(s, "gy", step) for s, step in zip(y_slabs, (1, -1))]
    fb, fw, matrix, z_a, z_b = call(functools.partial(z_pack_kernel, mesh_shape), frames)(*own, *parts, *y_parts)
    return fb, fw, matrix, ring(z_a, "gz", 1), ring(z_b, "gz", -1)


def shared_halo(mesh_shape, own, frames):
    tall, wide = own[0].shape[:2]
    tiles = own[2].shape[1] // 128
    strips, groups, per = (tiles + 7) // 8, tall // HALO, wide // 8
    z_shape = (groups * per + strips, HALO, 128)
    y_shape = (2 * tall + tiles, HALO, 128)
    x_shape = (2 * per * tall + tiles, HALO, 128)
    outs = [z_shape, z_shape, y_shape, y_shape, x_shape] + [a.shape for a in own]
    z_tail, z_head, y_tail, y_head, x_own, *here = call(face_kernel, outs, fetch=True)(*own)

    z_got = (ring(z_tail, "gz", 1), ring(z_head, "gz", -1))
    y_got = (ring(y_tail, "gy", 1), ring(y_head, "gy", -1))
    other = swap(x_own, "gx", 0)
    z_got = lax.optimization_barrier(z_got)
    edge = (2 * (groups + strips), HALO, 128)
    both = (2 * z_shape[0], HALO, 128)
    edge_tail, edge_head, z_both = call(functools.partial(y_edge_kernel, groups, per), [edge, edge, both])(*z_got)
    edge_got = (ring(edge_tail, "gy", 1), ring(edge_head, "gy", -1))
    z_other = swap(z_both, "gx", 0)
    y_other = [swap(y, "gx", 0) for y in y_got]
    edge_other = [swap(y, "gx", 0) for y in edge_got]
    return call(functools.partial(frame_kernel, mesh_shape), frames)(
        *here, other, *z_got, z_other, *y_got, *y_other, *edge_got, *edge_other
    )


def per_device(mesh_shape, sources, stiffness, coarse_inverse):
    n_gx, n_gy, n_gz = mesh_shape
    count = n_gx * n_gy * n_gz
    tall, wide, deep = stiffness.shape
    cells = coarse_inverse.shape[1]
    assert sources.shape[0] == 1 and deep == 128 and tall == 16 and wide == 16 and n_gz % 4 == 0 and cells % 128 == 0
    tiles = cells // 128
    extent = frame_extent(n_gx, tall)
    source = sources[0]
    own = (source, stiffness, coarse_inverse)
    rows = wide + 2 * HALO
    frame = (extent, rows, 128)
    z_slab = (extent // HALO + (tiles + 1) // 2, rows, 128)
    frames = [frame, frame, (9 * tiles, HALO, 128), z_slab, z_slab]
    exchange = shared_halo if n_gx == 2 else plain_halo
    fb, fw, matrix, z_a, z_b = exchange(mesh_shape, own, frames)
    padded = (extent + 2, rows + 16, 128)
    half, half_rows = extent // 2, rows // 2
    level1 = (half + 2, half_rows + 16, 128)
    window, face = (tall + 2, rows, 128), (tall, wide, 128)
    message = (count, wide // 2, 128)
    outs = [message, window, window, face, face, face] + [level1] * 6
    scratch = [padded] * 4 + [frame] + [(half, rows, 128)] * 4 + [(2, tall // 4, wide // 2, 128)]
    send, *state = call(functools.partial(down_kernel, mesh_shape), outs, scratch)(fb, fw, z_a, z_b)
    recv = lax.all_to_all(send, AXES, 0, 0, tiled=True)
    size_x, size_y, size_z = n_gx * tall // 4, n_gy * wide // 4, n_gz * deep // 4
    pad2 = (size_x + 2, size_y + 16, size_z)
    x3, rows3 = size_x // 2, size_y // 2
    pad3 = (x3 + 2, rows3 + 16, size_z)
    n2, lane_tiles = extent // 4, size_z // 128
    scratch = [
        pad2, (size_x, size_y, size_z), pad2, pad2, (size_x + 4, lane_tiles, size_y + 16, 128), (x3, lane_tiles, size_y, 128),
        (lane_tiles, size_y, 128), (lane_tiles, size_y, 128), pad3, (x3, rows3, size_z), pad3, pad3,
        (x3 // 2 + 2, lane_tiles, rows3 + 16, 128),
        (x3 // 2, rows3 // 2, size_z), (8, 128), level1, level1, (n2, 16, 128), (n2, 16, 128),
        (half, rows, 128), (half, rows, 128), window, face,
    ]
    (pressure,) = call(functools.partial(up_kernel, mesh_shape), [face], scratch, False)(recv, matrix, z_a, z_b, *state)
    return pressure[None]


def solution(mesh):
    mesh_shape = tuple(mesh.shape[a] for a in AXES)
    in_specs = (P(None, "gx", "gy", "gz"), P("gx", "gy", "gz"), P(AXES, None))
    return jax.shard_map(
        functools.partial(per_device, mesh_shape),
        mesh=mesh,
        in_specs=in_specs,
        out_specs=P(None, "gx", "gy", "gz"),
        check_vma=False,
    )
```

profile of v0, /device:TPU:0, one launch (start us, length us, event | category | flops | bytes accessed | tf_op | source)
XLA Modules:
  0.0 46.2 jit_solution(17063639587001940461)
XLA Ops:
  0.0 1.2 %shard_map.37 = (f32[5,8,128]{2,1,0:T(8,128)S(1)}, f32[5,8,128]{2,1,0:T(8,128)S(1)}, f32[34,8,128]{2,1,0:T(8,128)S(1)}, f32[34,8,128]{2,1,0:T(8,128)S(1)}, f32[6...) custom-call(f32[16,16,128]{2,1,0:T(8,128)} %bitcast.2, ...), custom_call_target="tpu_custom_call" | custom-call | tf_op jit(solution)/shard_map/pallas_call | solution.py:694
  1.2 3.0 %collective-permute-start.4 = (f32[34,8,128]{2,1,0:T(8,128)S(1)}, f32[34,8,128]{2,1,0:T(8,128)S(1)}, u32[]{:S(2)}, u32[]{:S(2)}) collective-permute-start(f32[34,8,128]{2,1,0:T(8,128)S(1)} %get-tuple-element.44), channel_id=1, source_target_pairs={{0,4},{4,8},{8,12},{12,0},{1,5},{5,9},{9,13},{13,1},{2,6},{6,10},{... | collective-permute-start | bytes 417800 | tf_op jit(solution)/shard_map/ppermute | solution.py:29
  4.2 1.0 %collective-permute-start.5 = (f32[34,8,128]{2,1,0:T(8,128)S(1)}, f32[34,8,128]{2,1,0:T(8,128)S(1)}, u32[]{:S(2)}, u32[]{:S(2)}) collective-permute-start(f32[34,8,128]{2,1,0:T(8,128)S(1)} %get-tuple-element.45), channel_id=1, source_target_pairs={{0,12},{4,0},{8,4},{12,8},{1,13},{5,1},{9,5},{13,9},{2,14},{6,2},{... | collective-permute-start | bytes 417800 | tf_op jit(solution)/shard_map/ppermute | solution.py:29
  5.2 0.0 collective-permute-start
  5.2 4.5 %collective-permute-done.4.refs_7_ = f32[34,8,128]{2,1,0:T(8,128)S(1)} collective-permute-done((f32[34,8,128]{2,1,0:T(8,128)S(1)}, f32[34,8,128]{2,1,0:T(8,128)S(1)}, u32[]{:S(2)}, u32[]{:S(2)}) %collective-permute-start.4) | collective-permute-done | bytes 139296 | tf_op jit(solution)/shard_map/ppermute | solution.py:29
  9.7 0.0 collective-permute-start.6
  9.7 2.4 %collective-permute-done.5.refs_8_ = f32[34,8,128]{2,1,0:T(8,128)S(1)} collective-permute-done((f32[34,8,128]{2,1,0:T(8,128)S(1)}, f32[34,8,128]{2,1,0:T(8,128)S(1)}, u32[]{:S(2)}, u32[]{:S(2)}) %collective-permute-start.5) | collective-permute-done | bytes 139296 | tf_op jit(solution)/shard_map/ppermute | solution.py:29
  12.1 0.0 collective-permute-start.7
  12.1 1.6 %collective-permute-start.1 = (f32[5,8,128]{2,1,0:T(8,128)S(1)}, f32[5,8,128]{2,1,0:T(8,128)S(1)}, u32[]{:S(2)}, u32[]{:S(2)}) collective-permute-start(f32[5,8,128]{2,1,0:T(8,128)S(1)} %get-tuple-element.39), channel_id=1, source_target_pairs={{0,1},{1,2},{2,3},{3,0},{4,5},{5,6},{6,7},{7,4},{8,9},{9,10},{10,1... | collective-permute-start | bytes 61448 | tf_op jit(solution)/shard_map/ppermute | solution.py:29
  13.7 2.2 %collective-permute-start.2 = (f32[5,8,128]{2,1,0:T(8,128)S(1)}, f32[5,8,128]{2,1,0:T(8,128)S(1)}, u32[]{:S(2)}, u32[]{:S(2)}) collective-permute-start(f32[5,8,128]{2,1,0:T(8,128)S(1)} %get-tuple-element.40), channel_id=1, source_target_pairs={{0,3},{1,0},{2,1},{3,2},{4,7},{5,4},{6,5},{7,6},{8,11},{9,8},{10,9... | collective-permute-start | bytes 61448 | tf_op jit(solution)/shard_map/ppermute | solution.py:29
  15.9 1.8 %collective-permute-done.1.refs_0_.refs_4_ = f32[5,8,128]{2,1,0:T(8,128)S(1)} collective-permute-done((f32[5,8,128]{2,1,0:T(8,128)S(1)}, f32[5,8,128]{2,1,0:T(8,128)S(1)}, u32[]{:S(2)}, u32[]{:S(2)}) %collective-permute-start.1) | collective-permute-done | bytes 20512 | tf_op jit(solution)/shard_map/ppermute | solution.py:29
  17.7 0.0 collective-permute-done.2.refs_1_.refs_5_
  17.7 1.5 %collective-permute-start.8 = (f32[6,8,128]{2,1,0:T(8,128)S(1)}, f32[6,8,128]{2,1,0:T(8,128)S(1)}, u32[]{:S(2)}, u32[]{:S(2)}) collective-permute-start(f32[6,8,128]{2,1,0:T(8,128)S(1)} %get-tuple-element.46), channel_id=1, source_target_pairs={{0,4},{4,8},{8,12},{12,0},{1,5},{5,9},{9,13},{13,1},{2,6},{6,10},{... | collective-permute-start | bytes 73736 | tf_op jit(solution)/shard_map/ppermute | solution.py:29
  19.3 0.0 collective-permute-start.3
  19.3 3.2 %collective-permute-done.8.refs_11_ = f32[6,8,128]{2,1,0:T(8,128)S(1)} collective-permute-done((f32[6,8,128]{2,1,0:T(8,128)S(1)}, f32[6,8,128]{2,1,0:T(8,128)S(1)}, u32[]{:S(2)}, u32[]{:S(2)}) %collective-permute-start.8) | collective-permute-done | bytes 24608 | tf_op jit(solution)/shard_map/ppermute | solution.py:29
  22.5 0.5 %collective-permute-start.9 = (f32[6,8,128]{2,1,0:T(8,128)S(1)}, f32[6,8,128]{2,1,0:T(8,128)S(1)}, u32[]{:S(2)}, u32[]{:S(2)}) collective-permute-start(f32[6,8,128]{2,1,0:T(8,128)S(1)} %get-tuple-element.47), channel_id=1, source_target_pairs={{0,12},{4,0},{8,4},{12,8},{1,13},{5,1},{9,5},{13,9},{2,14},{6,2},{... | collective-permute-start | bytes 73736 | tf_op jit(solution)/shard_map/ppermute | solution.py:29
  23.0 3.3 %collective-permute-done.9.refs_12_ = f32[6,8,128]{2,1,0:T(8,128)S(1)} collective-permute-done((f32[6,8,128]{2,1,0:T(8,128)S(1)}, f32[6,8,128]{2,1,0:T(8,128)S(1)}, u32[]{:S(2)}, u32[]{:S(2)}) %collective-permute-start.9) | collective-permute-done | bytes 24608 | tf_op jit(solution)/shard_map/ppermute | solution.py:29
  26.3 0.0 collective-permute-start.10
  26.3 0.0 collective-permute-done.3.refs_6_
  26.3 0.5 %collective-permute-start.11 = (f32[6,8,128]{2,1,0:T(8,128)S(1)}, f32[6,8,128]{2,1,0:T(8,128)S(1)}, u32[]{:S(2)}, u32[]{:S(2)}) collective-permute-start(f32[6,8,128]{2,1,0:T(8,128)S(1)} %collective-permute-done.9.refs_12_), channel_id=1, source_target_pairs={{0,16},{16,0},{1,17},{17,1},{2,18},{18,2},{3,19},{19,3},{4,20},{20... | collective-permute-start | bytes 73736 | tf_op jit(solution)/shard_map/ppermute | solution.py:24
  26.8 0.7 %collective-permute-done.10.refs_13_ = f32[6,8,128]{2,1,0:T(8,128)S(1)} collective-permute-done((f32[6,8,128]{2,1,0:T(8,128)S(1)}, f32[6,8,128]{2,1,0:T(8,128)S(1)}, u32[]{:S(2)}, u32[]{:S(2)}) %collective-permute-start.10) | collective-permute-done | bytes 24608 | tf_op jit(solution)/shard_map/ppermute | solution.py:24
  27.5 0.2 collective-permute-done.11.refs_14_
  27.7 0.0 collective-permute-done.refs_3_
  27.7 0.0 collective-permute-done.6.refs_9_
  27.7 0.0 collective-permute-done.7.refs_10_
  27.7 0.1 shard_map.39
  27.8 3.1 %shard_map.40 = (f32[32,8,128]{2,1,0:T(8,128)S(1)}, f32[18,32,128]{2,1,0:T(8,128)S(1)}, f32[18,32,128]{2,1,0:T(8,128)S(1)}, f32[16,16,128]{2,1,0:T(8,128)S(1)}, ...) custom-call(f32[24,32,128]{2,1,0:T(8,128)S(1)} %get-tuple-element.48, ...), custom_call_target="tpu_custom_call" | custom-call | tf_op jit(solution)/shard_map/pallas_call | solution.py:694
  31.0 12.9 %all_to_all.5.refs_0_ = f32[32,8,128]{2,1,0:T(8,128)S(1)} all-to-all(f32[32,8,128]{2,1,0:T(8,128)S(1)} %get-tuple-element.52), channel_id=1, replica_groups=mesh['gx'=2,'gy'=4,'gz'=4] {'gx','gy','gz'}, dimensions={0} | all-to-all | bytes 262144 | tf_op jit(solution)/shard_map/all_to_all | solution.py:765
  43.8 2.4 %shard_map.41 = f32[16,16,128]{2,1,0:T(8,128)} custom-call(f32[32,8,128]{2,1,0:T(8,128)S(1)} %all_to_all.5.refs_0_, f32[18,8,128]{2,1,0:T(8,128)S(1)} %get-tuple-element.53.refs_1_, f32[4,32,128]{2,1,0:T(8,128)S(1)} %get-tuple-element.50.refs_2_, f32[4,32,128]{2,1,0:T(8,128)S(1)} %get-tuple-element.51.refs_3_, f32[18,32,128]{2,1,0:T(8,128)S(1)} %get-tuple-element.54.refs_4_, ...), custom_call_target="tpu_custom_call" | custom-call | tf_op jit(solution)/shard_map/pallas_call | solution.py:694
  (1 shorter events, 0.0 us)
Async XLA Ops:
  1.2 8.5 %collective-permute-start.4 = (f32[34,8,128]{2,1,0:T(8,128)S(1)}, f32[34,8,128]{2,1,0:T(8,128)S(1)}, u32[]{:S(2)}, u32[]{:S(2)}) collective-permute-start(f32[34,8,128]{2,1,0:T(8,128)S(1)} %get-tuple-element.44), channel_id=1, source_target_pairs={{0,4},{4,8},{8,12},{12,0},{1,5},{5,9},{9,13},{13,1},{2,6},{6,10},{... | collective-permute-start | bytes 417800 | tf_op jit(solution)/shard_map/ppermute | solution.py:29
  4.2 7.9 %collective-permute-start.5 = (f32[34,8,128]{2,1,0:T(8,128)S(1)}, f32[34,8,128]{2,1,0:T(8,128)S(1)}, u32[]{:S(2)}, u32[]{:S(2)}) collective-permute-start(f32[34,8,128]{2,1,0:T(8,128)S(1)} %get-tuple-element.45), channel_id=1, source_target_pairs={{0,12},{4,0},{8,4},{12,8},{1,13},{5,1},{9,5},{13,9},{2,14},{6,2},{... | collective-permute-start | bytes 417800 | tf_op jit(solution)/shard_map/ppermute | solution.py:29
  5.2 22.4 %collective-permute-start = (f32[66,8,128]{2,1,0:T(8,128)S(1)}, f32[66,8,128]{2,1,0:T(8,128)S(1)}, u32[]{:S(2)}, u32[]{:S(2)}) collective-permute-start(f32[66,8,128]{2,1,0:T(8,128)S(1)} %get-tuple-element.38), channel_id=1, source_target_pairs={{0,16},{16,0},{1,17},{17,1},{2,18},{18,2},{3,19},{19,3},{4,20},{20... | collective-permute-start | bytes 811016 | tf_op jit(solution)/shard_map/ppermute | solution.py:24
  9.7 18.0 %collective-permute-start.6 = (f32[34,8,128]{2,1,0:T(8,128)S(1)}, f32[34,8,128]{2,1,0:T(8,128)S(1)}, u32[]{:S(2)}, u32[]{:S(2)}) collective-permute-start(f32[34,8,128]{2,1,0:T(8,128)S(1)} %collective-permute-done.4.refs_7_), channel_id=1, source_target_pairs={{0,16},{16,0},{1,17},{17,1},{2,18},{18,2},{3,19},{19,3},{4,20},{20... | collective-permute-start | bytes 417800 | tf_op jit(solution)/shard_map/ppermute | solution.py:24
  12.1 15.6 %collective-permute-start.7 = (f32[34,8,128]{2,1,0:T(8,128)S(1)}, f32[34,8,128]{2,1,0:T(8,128)S(1)}, u32[]{:S(2)}, u32[]{:S(2)}) collective-permute-start(f32[34,8,128]{2,1,0:T(8,128)S(1)} %collective-permute-done.5.refs_8_), channel_id=1, source_target_pairs={{0,16},{16,0},{1,17},{17,1},{2,18},{18,2},{3,19},{19,3},{4,20},{20... | collective-permute-start | bytes 417800 | tf_op jit(solution)/shard_map/ppermute | solution.py:24
  12.1 5.6 %collective-permute-start.1 = (f32[5,8,128]{2,1,0:T(8,128)S(1)}, f32[5,8,128]{2,1,0:T(8,128)S(1)}, u32[]{:S(2)}, u32[]{:S(2)}) collective-permute-start(f32[5,8,128]{2,1,0:T(8,128)S(1)} %get-tuple-element.39), channel_id=1, source_target_pairs={{0,1},{1,2},{2,3},{3,0},{4,5},{5,6},{6,7},{7,4},{8,9},{9,10},{10,1... | collective-permute-start | bytes 61448 | tf_op jit(solution)/shard_map/ppermute | solution.py:29
  13.7 4.0 %collective-permute-start.2 = (f32[5,8,128]{2,1,0:T(8,128)S(1)}, f32[5,8,128]{2,1,0:T(8,128)S(1)}, u32[]{:S(2)}, u32[]{:S(2)}) collective-permute-start(f32[5,8,128]{2,1,0:T(8,128)S(1)} %get-tuple-element.40), channel_id=1, source_target_pairs={{0,3},{1,0},{2,1},{3,2},{4,7},{5,4},{6,5},{7,6},{8,11},{9,8},{10,9... | collective-permute-start | bytes 61448 | tf_op jit(solution)/shard_map/ppermute | solution.py:29
  17.7 4.8 %collective-permute-start.8 = (f32[6,8,128]{2,1,0:T(8,128)S(1)}, f32[6,8,128]{2,1,0:T(8,128)S(1)}, u32[]{:S(2)}, u32[]{:S(2)}) collective-permute-start(f32[6,8,128]{2,1,0:T(8,128)S(1)} %get-tuple-element.46), channel_id=1, source_target_pairs={{0,4},{4,8},{8,12},{12,0},{1,5},{5,9},{9,13},{13,1},{2,6},{6,10},{... | collective-permute-start | bytes 73736 | tf_op jit(solution)/shard_map/ppermute | solution.py:29
  19.3 7.1 %collective-permute-start.3 = (f32[10,8,128]{2,1,0:T(8,128)S(1)}, f32[10,8,128]{2,1,0:T(8,128)S(1)}, u32[]{:S(2)}, u32[]{:S(2)}) collective-permute-start(f32[10,8,128]{2,1,0:T(8,128)S(1)} %get-tuple-element.43), channel_id=1, source_target_pairs={{0,16},{16,0},{1,17},{17,1},{2,18},{18,2},{3,19},{19,3},{4,20},{20... | collective-permute-start | bytes 122888 | tf_op jit(solution)/shard_map/ppermute | solution.py:24
  22.5 3.8 %collective-permute-start.9 = (f32[6,8,128]{2,1,0:T(8,128)S(1)}, f32[6,8,128]{2,1,0:T(8,128)S(1)}, u32[]{:S(2)}, u32[]{:S(2)}) collective-permute-start(f32[6,8,128]{2,1,0:T(8,128)S(1)} %get-tuple-element.47), channel_id=1, source_target_pairs={{0,12},{4,0},{8,4},{12,8},{1,13},{5,1},{9,5},{13,9},{2,14},{6,2},{... | collective-permute-start | bytes 73736 | tf_op jit(solution)/shard_map/ppermute | solution.py:29
  26.3 1.2 %collective-permute-start.10 = (f32[6,8,128]{2,1,0:T(8,128)S(1)}, f32[6,8,128]{2,1,0:T(8,128)S(1)}, u32[]{:S(2)}, u32[]{:S(2)}) collective-permute-start(f32[6,8,128]{2,1,0:T(8,128)S(1)} %collective-permute-done.8.refs_11_), channel_id=1, source_target_pairs={{0,16},{16,0},{1,17},{17,1},{2,18},{18,2},{3,19},{19,3},{4,20},{20... | collective-permute-start | bytes 73736 | tf_op jit(solution)/shard_map/ppermute | solution.py:24
  26.3 1.4 %collective-permute-start.11 = (f32[6,8,128]{2,1,0:T(8,128)S(1)}, f32[6,8,128]{2,1,0:T(8,128)S(1)}, u32[]{:S(2)}, u32[]{:S(2)}) collective-permute-start(f32[6,8,128]{2,1,0:T(8,128)S(1)} %collective-permute-done.9.refs_12_), channel_id=1, source_target_pairs={{0,16},{16,0},{1,17},{17,1},{2,18},{18,2},{3,19},{19,3},{4,20},{20... | collective-permute-start | bytes 73736 | tf_op jit(solution)/shard_map/ppermute | solution.py:24
where the time goes:
time: 46.4 us; the launch traced here: 46.2 us
  waiting for transfers between devices  16 us (34%)
  blocking collectives  12.9 us (28%)
  starting transfers between devices  10.5 us (23%)
  Pallas kernels  6.88 us (15%)
    ppermute x6, waiting for transfers between devices, ring(): lax.ppermute(values, axis, [(i, (i + step) % count) for i in range(count)])  15.1 us
    all_to_all x1, blocking collectives, per_device(): recv = lax.all_to_all(send, AXES, 0, 0, tiled=True)  12.9 us
    ppermute x6, starting transfers between devices, ring(): lax.ppermute(values, axis, [(i, (i + step) % count) for i in range(count)])  9.94 us
    pallas_call x5, Pallas kernels, call(): return lambda *values: run(*map(place, values))  6.88 us
  transfers between devices with their start and end apart: 12, of which 7 were waited for; matrix products, arithmetic and copies ran while one was open for 0% of the time, Pallas kernels for 0%

commit v1 on v0

--- a/solution.py
+++ b/solution.py
@@ -82,6 +82,16 @@
 
 def inverse(weights):
     return jnp.where(weights > 0.0, 1.0 / jnp.where(weights > 0.0, weights, 1.0), 0.0)
+
+
+def select_lanes(values, chosen):
+    first = values.astype(jnp.bfloat16)
+    rest = values - first.astype(F32)
+    second = rest.astype(jnp.bfloat16)
+    third = (rest - second.astype(F32)).astype(jnp.bfloat16)
+    matrix = chosen.astype(F32).astype(jnp.bfloat16)
+    parts = [jnp.dot(p, matrix, preferred_element_type=F32) for p in (first, second, third)]
+    return parts[0] + (parts[1] + parts[2])
 
 
 def tiled(value):
@@ -138,6 +148,13 @@
 def y_ends(count, wide):
     index = lax.axis_index("gy")
     return (dict(valid=index > 0, place=0, high=0), dict(valid=index < count - 1, place=wide + HALO, high=1))
+
+
+def inner_frames(padded, plain):
+    extent, rows = plain.shape[0], plain.shape[1]
+    for x in (0, extent + 1):
+        padded[x] = jnp.zeros(padded.shape[1:], F32)
+    return padded.at[pl.ds(1, extent), pl.ds(8, rows), :], plain
 
 
 def frame_extent(count, tall):
@@ -178,7 +195,7 @@
     n_in = 3 * (1 + min(n_gx - 1, 2))
     own_refs, part_refs = refs[:3], refs[3:n_in]
     y_refs = refs[n_in : n_in + 2]
-    frames = refs[n_in + 2 : n_in + 4]
+    frames = inner_frames(*refs[n_in + 2 : n_in + 4])
     rows_ref, z_outs = refs[n_in + 4], refs[n_in + 5 :]
     tall, wide = own_refs[0].shape[0], own_refs[0].shape[1]
     extent = frame_extent(n_gx, tall)
@@ -230,15 +247,21 @@
         packed = jnp.zeros((rows, 128), F32)
         for i in range(HALO):
             for a in range(2):
-                piece = roll(frames[a][group * HALO + i], 8 * (tail + 2 * i + a))
-                packed = jnp.where(slot == 2 * i + a, piece, packed)
+                at = (2 * i + a + 1 - tail) % 16
+                piece = roll(frames[a][group * HALO + i], 8 * (tail + at))
+                packed = jnp.where(slot == at, piece, packed)
         out(group, packed)
 
 
 def face_kernel(*refs):
-    b, w, matrix, *outs = refs
-    outs, y_outs, both, copies = outs[:2], outs[2:4], outs[4], outs[5:]
+    source, weights, matrix, *outs = refs
+    outs, y_outs, both, (b, w, own_matrix, own_inverse) = outs[:2], outs[2:4], outs[4], outs[5:]
     tall, wide = b.shape[0], b.shape[1]
+    inverses = 1.0 / weights[...]
+    own_inverse[...] = inverses
+    b[...] = K * source[...] * inverses
+    w[...] = weights[...]
+    own_matrix[...] = matrix[...]
     tiles = matrix.shape[1] // 128
     strips = (tiles + 7) // 8
     per = wide // 8
@@ -267,8 +290,6 @@
             at += tall
     for t in range(tiles):
         both[at + t] = matrix[:, t * 128 : (t + 1) * 128]
-    for ref, copy in zip((b, w, matrix), copies):
-        copy[...] = ref[...]
 
 
 def y_edge_kernel(groups, per, *refs):
@@ -289,7 +310,7 @@
     n_gx, n_gy, _ = mesh_shape
     own_refs, other, z_refs, z_other = refs[:3], refs[3], refs[4:6], refs[6]
     y_refs, y_others, edge_refs, edge_others = refs[7:9], refs[9:11], refs[11:13], refs[13:15]
-    frames, rows_ref, z_outs = refs[15:17], refs[17], refs[18:]
+    frames, rows_ref, z_outs = inner_frames(*refs[15:17]), refs[17], refs[18:]
     tall, wide = own_refs[0].shape[0], own_refs[0].shape[1]
     extent = frame_extent(n_gx, tall)
     tiles = own_refs[2].shape[1] // 128
@@ -350,87 +371,87 @@
 
 
 def down_kernel(mesh_shape, *refs):
-    n_gx, _, n_gz = mesh_shape
-    fb, fw, za, zb = refs[:4]
-    send, v0w, w0w, v0h, w0h, g0, v1m, v1s, w1m, w1s, g1m, g1s = refs[4:16]
-    gm, gs, vm, vs, ws, tm, ts, um, us, small = refs[16:]
-    extent, rows = fb.shape[0], fb.shape[1]
-    tall = g0.shape[0]
-    wide = g0.shape[1]
+    n_gx, n_gy, n_gz = mesh_shape
+    gm, fw, za, zb = refs[:4]
+    send, vm, gs, vs, ws, v1m, v1s, w1m, w1s, g1m, g1s, i1m, i1s = refs[4:17]
+    tm, ts, um, us, small = refs[17:]
+    extent, rows = fw.shape[0], fw.shape[1]
+    tall, wide = extent - frame_extent(n_gx, 0), rows - 2 * HALO
     half, half_rows = extent // 2, rows // 2
-    _, own, _ = x_frame(n_gx, tall)
+    ix, own, _ = x_frame(n_gx, tall)
     groups = extent // HALO
-    zero = jnp.zeros((8, 128), F32)
-
-    def clear(ref, count, depth):
-        for x in (0, count + 1):
-            for r in range(0, depth + 16, 8):
-                ref[x, r : r + 8, :] = zero
-        for x in range(1, count + 1):
-            ref[x, 0:8, :] = zero
-            ref[x, depth + 8 : depth + 16, :] = zero
-
-    for ref in (gm, gs, vm, vs):
-        clear(ref, extent, rows)
-    for ref in (v1m, v1s, g1m, g1s, w1m, w1s):
-        clear(ref, half, half_rows)
+    for ref in (gs, vm, vs, g1m, g1s, v1m, v1s):
+        for x in (0, ref.shape[0] - 1):
+            ref[x] = jnp.zeros(ref.shape[1:], F32)
+
+    ends, sides = z_ends(n_gz), y_ends(n_gy, wide)
+
+    def inside(depth, step):
+        row, lane = iota((depth, 128), 0), iota((depth, 128), 1)
+        edge = HALO // step
+        low, high = ((e["valid"].astype(F32)) for e in sides)
+        main = jnp.where(row < edge, K * low, jnp.where(row >= depth - edge, K * high, K))
+        low, high = (e["valid"].astype(F32) for e in ends)
+        return main, main * jnp.where(lane >= 120, low, jnp.where(lane < HALO, high, 0.0))
+
+    def present(x, step):
+        if n_gx <= 2:
+            return None
+        edge = HALO // step
+        out = ((x < edge) & (ix == 0)) | ((x >= extent // step - edge) & (ix == n_gx - 1))
+        return 1.0 - out.astype(F32)
 
     lane = iota((rows, 128), 1)
-    ends = z_ends(n_gz)
-    masks = [((lane >= e["lane"]) & (lane < e["lane"] + HALO)).astype(F32) * e["valid"].astype(F32) for e in ends]
+    halo_lanes = jnp.where(lane >= 120, ends[0]["valid"].astype(F32), 0.0) + jnp.where(lane < HALO, ends[1]["valid"].astype(F32), 0.0)
+    first_half = lane % 16 < HALO
 
     def load(group):
+        low, high = za[group], zb[group]
+        both = (jnp.where(first_half, low, high), jnp.where(first_half, high, low))
         for i in range(HALO):
             x = group * HALO + i
-            sides = []
-            for a in range(2):
-                total = None
-                for ref, mask, end in zip((za, zb), masks, ends):
-                    piece = roll(ref[group], end["lane"] - 16 * i - 8 * a) * mask
-                    total = piece if total is None else total + piece
-                sides.append(total)
-            ws[x] = sides[1]
-            gm[x + 1, 8 : 8 + rows, :] = K * fb[x] * inverse(fw[x])
-            gs[x + 1, 8 : 8 + rows, :] = K * sides[0] * inverse(sides[1])
+            gs[x + 1, 8 : 8 + rows, :] = roll(both[0], 120 - 16 * i) * halo_lanes
+            ws[x] = roll(both[1], 112 - 16 * i) * halo_lanes
 
     each(groups, load, 4)
 
-    def second(x):
-        main, side, main_n, side_n = neighbours(gm, gs, x + 1, 8, rows, 1)
-        vm[x + 1, 8 : 8 + rows, :] = 1.2 * main + jnp.where(fw[x] > 0.0, K * main_n, 0.0)
-        vs[x + 1, 8 : 8 + rows, :] = 1.2 * side + jnp.where(ws[x] > 0.0, K * side_n, 0.0)
-
-    each(extent, second, 8)
+    def smooth(g_refs, v_refs, factors, x, depth, step):
+        main, side, main_n, side_n = neighbours(*g_refs, x + 1, 8, depth, step)
+        here = present(x, step)
+        for ref, value, near, factor in zip(v_refs, (main, side), (main_n, side_n), factors):
+            ref[x + 1, 8 : 8 + depth, :] = 1.2 * value + (factor if here is None else factor * here) * near
+
+    factors = inside(rows, 1)
+    each(extent, lambda x: smooth((gm, gs), (vm, vs), factors, x, rows, 1), 24)
 
     def residual(x2):
-        totals = None
-        for j in range(2):
-            x = 2 * x2 + j
-            main, side, main_n, side_n = neighbours(vm, vs, x + 1, 8, rows, 1)
-            w_main, w_side = fw[x], ws[x]
-            r_main = w_main * ((1.0 / K) * gm[x + 1, 8 : 8 + rows, :] - 6.0 * main + main_n)
-            r_side = w_side * ((1.0 / K) * gs[x + 1, 8 : 8 + rows, :] - 6.0 * side + side_n)
-            values = (r_main, r_side, w_main, w_side)
-            totals = values if j == 0 else tuple(a + b for a, b in zip(totals, values))
-        for ref, value in zip((tm, ts, um, us), totals):
-            ref[x2] = value
+        for row in range(0, rows, 8):
+            totals = None
+            for j in range(2):
+                x = 2 * x2 + j
+                main, side, main_n, side_n = neighbours(vm, vs, x + 1, 8 + row, 8, 1)
+                w_main, w_side = fw[x, row : row + 8, :], ws[x, row : row + 8, :]
+                r_main = w_main * ((1.0 / K) * gm[x + 1, 8 + row : 16 + row, :] - 6.0 * main + main_n)
+                r_side = w_side * ((1.0 / K) * gs[x + 1, 8 + row : 16 + row, :] - 6.0 * side + side_n)
+                values = (r_main, r_side, w_main, w_side)
+                totals = values if j == 0 else tuple(a + b for a, b in zip(totals, values))
+            for ref, value in zip((tm, ts, um, us), totals):
+                ref[x2, row : row + 8, :] = value
 
         def pairs(ref):
             return lane_pairs(ref[x2, pl.ds(0, half_rows, stride=2), :] + ref[x2, pl.ds(1, half_rows, stride=2), :], 1)
 
-        for t_ref, u_ref, w_out, g_out in ((tm, um, w1m, g1m), (ts, us, w1s, g1s)):
+        for t_ref, u_ref, w_out, g_out, i_out in ((tm, um, w1m, g1m, i1m), (ts, us, w1s, g1s, i1s)):
             weights = 0.0625 * pairs(u_ref)
-            w_out[x2 + 1, 8 : 8 + half_rows, :] = weights
-            g_out[x2 + 1, 8 : 8 + half_rows, :] = (0.125 * K) * pairs(t_ref) * inverse(weights)
-
-    each(half, residual, 4)
-
-    def second_1(x):
-        main, side, main_n, side_n = neighbours(g1m, g1s, x + 1, 8, half_rows, 2)
-        v1m[x + 1, 8 : 8 + half_rows, :] = 1.2 * main + jnp.where(w1m[x + 1, 8 : 8 + half_rows, :] > 0.0, K * main_n, 0.0)
-        v1s[x + 1, 8 : 8 + half_rows, :] = 1.2 * side + jnp.where(w1s[x + 1, 8 : 8 + half_rows, :] > 0.0, K * side_n, 0.0)
-
-    each(half, second_1, 16)
+            inverses = inverse(weights)
+            w_out[x2, :, :] = weights
+            i_out[x2, :, :] = inverses
+            g_out[x2 + 1, 8 : 8 + half_rows, :] = (0.125 * K) * pairs(t_ref) * inverses
+
+    each(half, residual, 12)
+
+    factors_1 = inside(half_rows, 2)
+    each(half, lambda x: smooth((g1m, g1s), (v1m, v1s), factors_1, x, half_rows, 2), 16)
 
     base = own // 2
     first_row = 8 + HALO // 2
@@ -440,7 +461,7 @@
         for j in range(2):
             x = base + 2 * x2 + j + 1
             main, _, main_n, _ = neighbours(v1m, v1s, x, first_row, wide // 2, 2)
-            weights = w1m[x, pl.ds(first_row, wide // 2), :]
+            weights = w1m[x - 1, pl.ds(first_row - 8, wide // 2), :]
             res = weights * ((1.0 / K) * g1m[x, pl.ds(first_row, wide // 2), :] - 6.0 * main + main_n)
             total_r = res if j == 0 else total_r + res
             total_w = weights if j == 0 else total_w + weights
@@ -451,11 +472,11 @@
         for x2 in range(quarter):
             ref = small.at[a, x2]
             both = ref[pl.ds(0, quarter_rows, stride=2), :] + ref[pl.ds(1, quarter_rows, stride=2), :]
-            q.append(factor * lane_pairs(both, 2))
+            q.append(factor * both)
     stacked = jnp.concatenate([jnp.concatenate(q[:quarter], axis=0), jnp.concatenate(q[quarter:], axis=0)], axis=0)
     src, dst = iota((128, 128), 0), iota((128, 128), 1)
-    pick = (src == 4 * (dst % 32)).astype(F32)
-    compact = jnp.dot(stacked, pick, precision=lax.Precision.HIGHEST, preferred_element_type=F32)
+    cell = 4 * (dst % 32)
+    compact = select_lanes(stacked, (src == cell) | (src == cell + 2))
     block = iota((quarter_rows, 128), 1) // 32
     gz = lax.axis_index("gz")
     out = []
@@ -472,21 +493,11 @@
 
     each(send.shape[0], copy, 8)
 
-    for i in range(tall + 2):
-        v0w[i] = vm[own + i, 8 : 8 + rows, :]
-        x = own + (i - 1)
-        inside = (x >= 0) & (x < extent)
-        w0w[i] = keep(inside, fw[jnp.clip(x, 0, extent - 1)])
-    for i in range(tall):
-        v0h[i] = vs[own + i + 1, 8 + HALO : 8 + HALO + wide, :]
-        w0h[i] = ws[own + i, HALO : HALO + wide, :]
-        g0[i] = gm[own + i + 1, 8 + HALO : 8 + HALO + wide, :]
-
 
 def up_kernel(mesh_shape, *refs):
     n_gx, n_gy, n_gz = mesh_shape
-    recv, rows_ref, za, zb, v0w, w0w, v0h, w0h, g0, v1m, v1s, w1m, w1s, g1m, g1s, out = refs[:16]
-    g2, w2, v2, y2, e2, p2, t3, u3, g3, w3, v3, y3, p3, b4, _, y1m, y1s, e1m, e1s, f1m, f1s, y0m, y0s = refs[16:]
+    recv, rows_ref, za, zb, gm, fw, i0, vm, _, vs, ws, v1m, v1s, w1m, w1s, g1m, g1s, i1m, i1s, out = refs[:20]
+    g2, w2, i2, v2, y2, e2, p2, t3, u3, g3, w3, i3, v3, y3, p3, b4, y1m, y1s, e1m, e1s, f1m, f1s, y0m, y0s = refs[20:]
     tall, wide = out.shape[0], out.shape[1]
     size_x, size_z = w2.shape[0], w2.shape[2]
     size_y = w2.shape[1]
@@ -494,7 +505,7 @@
     iy, iz = lax.axis_index("gy"), lax.axis_index("gz")
     quarter, quarter_rows = tall // 4, wide // 4
     extent = frame_extent(n_gx, tall)
-    half, half_rows = v1m.shape[0] - 2, v1m.shape[1] - 16
+    half, half_rows = w1m.shape[0], w1m.shape[1]
 
     def clear(ref):
         count, depth, size = ref.shape
@@ -528,8 +539,10 @@
                     tiles_b.append(roll(picked[0], -32 * x))
                     tiles_w.append(roll(picked[1], -32 * x))
                 weights = joined(tiles_w)
+                inverses = 1.0 / weights
                 w2[gx * quarter + x, gy * quarter_rows : (gy + 1) * quarter_rows, :] = weights
-                g2[gx * quarter + x + 1, 8 + gy * quarter_rows : 8 + (gy + 1) * quarter_rows, :] = K * joined(tiles_b) / weights
+                i2[gx * quarter + x, gy * quarter_rows : (gy + 1) * quarter_rows, :] = inverses
+                g2[gx * quarter + x + 1, 8 + gy * quarter_rows : 8 + (gy + 1) * quarter_rows, :] = K * joined(tiles_b) * inverses
 
     def smooth(g, v, x, rows, step):
         main, near = global_neighbours(g, x + 1, 8, rows, step)
@@ -549,8 +562,10 @@
             u3[t] = part
         pairs = lambda ref: lane_pairs(row_pairs(ref, size_y), 1)
         weights = 0.0625 * pairs(u3)
+        inverses = 1.0 / weights
         w3[x] = weights
-        g3[x + 1, 8 : 8 + rows3, :] = (0.125 * K) * pairs(t3) / weights
+        i3[x] = inverses
+        g3[x + 1, 8 : 8 + rows3, :] = (0.125 * K) * pairs(t3) * inverses
 
     each(x3, restrict_2, 4)
     each(x3, lambda x: smooth(g3, v3, x, rows3, 2), 8)
@@ -559,7 +574,7 @@
     def restrict_3(x):
         for t, part in enumerate(tiled(resid(g3, v3, w3, 2 * x, rows3, 2) + resid(g3, v3, w3, 2 * x + 1, rows3, 2))):
             t3[t, 0:rows3, :] = part
-        b4[x] = 0.125 * lane_pairs(row_pairs(t3, rows3), 2)
+        b4[x] = 0.125 * row_pairs(t3, rows3)
 
     each(x4, restrict_3, 4)
 
@@ -567,9 +582,9 @@
     coarse_z = size_z // 4
     per = 128 // coarse_z
     src, dst = iota((size_z, 128), 0), iota((size_z, 128), 1)
-    pick = (src == 4 * (dst % coarse_z)).astype(F32)
     values = b4[0] if x4 == 1 else jnp.concatenate([b4[x] for x in range(x4)], axis=0)
-    compact = jnp.dot(values, pick, precision=lax.Precision.HIGHEST, preferred_element_type=F32)
+    cell = 4 * (dst % coarse_z)
+    compact = select_lanes(values, (src == cell) | (src == cell + 2))
     place = iota((x4 * rows4, 128), 0) % per == iota((x4 * rows4, 128), 1) // coarse_z
     compact = jnp.where(place, compact, 0.0)
     vectors = [jnp.sum(compact[t * per : (t + 1) * per], axis=0, keepdims=True) for t in range(tiles)]
@@ -606,14 +621,14 @@
         coarse = joined([p[px, t, row : row + rows, :] for t in range(p.shape[1])])
         y[x + 1, 8 : 8 + rows, :] = v[x + 1, 8 : 8 + rows, :] + w[x] * coarse
 
-    def relax(y, g, w, x, rows, step):
+    def relax(y, g, inverses, x, rows, step):
         main, near = global_neighbours(y, x + 1, 8, rows, step)
-        return (0.2 * main + g[x + 1, 8 : 8 + rows, :] + K * near) / w[x]
+        return (0.2 * main + g[x + 1, 8 : 8 + rows, :] + K * near) * inverses[x]
 
     each(x3, lambda x: lift(y3, v3, w3, p3, x, x // 2 + 1, rows3, 8), 8)
 
     def up_3(x):
-        for t, e3 in enumerate(tiled(relax(y3, g3, w3, x, rows3, 2))):
+        for t, e3 in enumerate(tiled(relax(y3, g3, i3, x, rows3, 2))):
             p2[x, t, pl.ds(0, rows3, stride=2), :] = e3
             p2[x, t, pl.ds(1, rows3, stride=2), :] = e3
 
@@ -621,7 +636,7 @@
     each(size_x, lambda x: lift(y2, v2, w2, p2, x, x // 2, size_y, 0), 8)
 
     def up_2(x):
-        for t, part in enumerate(tiled(relax(y2, g2, w2, x, size_y, 1))):
+        for t, part in enumerate(tiled(relax(y2, g2, i2, x, size_y, 1))):
             e2[x + 2, t, 8 : 8 + size_y, :] = part
 
     each(size_x, up_2, 8)
@@ -629,47 +644,56 @@
     src, dst = iota((size_z, 256), 0), iota((size_z, 256), 1)
     start = iz * 32
     cell = jnp.where(dst < 128, dst // 4, jnp.where(dst < 192, 32 + (dst - 128) // 4, -1 - (255 - dst) // 4))
-    widen = (src == start + cell).astype(F32)
+    widen = src == start + cell
     n2 = extent // 4
     x_start = ix * quarter - own // 4
     y_start = 8 + iy * quarter_rows - HALO // 4
     spread = None
     for t in range(size_z // 128):
         stacked = jnp.concatenate([e2[x_start + 2 + i, t, pl.ds(y_start, 8), :] for i in range(n2)], axis=0)
-        part = jnp.dot(stacked, widen[t * 128 : (t + 1) * 128], precision=lax.Precision.HIGHEST, preferred_element_type=F32)
+        part = select_lanes(stacked, widen[t * 128 : (t + 1) * 128])
         spread = part if spread is None else spread + part
     for i in range(n2):
         for ref, part in ((e1m, spread[i * 8 : i * 8 + 8, :128]), (e1s, spread[i * 8 : i * 8 + 8, 128:])):
             ref[i, pl.ds(0, 8, stride=2), :] = part
             ref[i, pl.ds(1, 8, stride=2), :] = part
 
-    clear(y1m)
-    clear(y1s)
+    for ref in (y1m, y1s):
+        for x in (0, half + 1):
+            ref[x] = jnp.zeros(ref.shape[1:], F32)
     inner = slice(8, 8 + half_rows)
     for x in range(half):
-        y1m[x + 1, inner, :] = v1m[x + 1, inner, :] + w1m[x + 1, inner, :] * e1m[x // 2]
-        y1s[x + 1, inner, :] = v1s[x + 1, inner, :] + w1s[x + 1, inner, :] * e1s[x // 2]
+        y1m[x + 1, inner, :] = v1m[x + 1, inner, :] + w1m[x] * e1m[x // 2]
+        y1s[x + 1, inner, :] = v1s[x + 1, inner, :] + w1s[x] * e1s[x // 2]
 
     def up_1(x):
         main, side, main_n, side_n = neighbours(y1m, y1s, x + 1, 8, half_rows, 2)
-        for f, y, near, g, w in ((f1m, main, main_n, g1m, w1m), (f1s, side, side_n, g1s, w1s)):
-            e1 = (0.2 * y + g[x + 1, inner, :] + K * near) * inverse(w[x + 1, inner, :])
+        for f, y, near, g, inverses in ((f1m, main, main_n, g1m, i1m), (f1s, side, side_n, g1s, i1s)):
+            e1 = (0.2 * y + g[x + 1, inner, :] + K * near) * inverses[x]
             f[x, pl.ds(0, half_rows, stride=2), :] = e1
             f[x, pl.ds(1, half_rows, stride=2), :] = e1
 
     each(half, up_1, 12)
     base = own // 2
+    extent_rows = fw.shape[1]
     for i in range(tall + 2):
         parent = jnp.clip(base + (i + 1) // 2 - 1, 0, half - 1)
-        y0m[i] = v0w[i] + w0w[i] * f1m[parent]
-        if 0 < i <= tall:
-            y0s[i - 1] = v0h[i - 1] + w0h[i - 1] * f1s[parent, HALO : HALO + wide, :]
+        x = own + (i - 1)
+        weights = fw[jnp.clip(x, 0, extent - 1)] if i in (0, tall + 1) else fw[x]
+        value = vm[x + 1, 8 : 8 + extent_rows, :] + weights * f1m[parent]
+        if i in (0, tall + 1):
+            value = keep((x >= 0) & (x < extent), value)
+        else:
+            y0s[i - 1] = (
+                vs[x + 1, 8 + HALO : 8 + HALO + wide, :] + ws[x, HALO : HALO + wide, :] * f1s[parent, HALO : HALO + wide, :]
+            )
+        y0m[i] = value
 
     def up_0(i):
         main = y0m[i + 1, pl.ds(HALO, wide), :]
         main_z, _ = z_sum(main, y0s[i], 1)
         near = xy_sum(y0m, i + 1, HALO, wide) + main_z
-        out[i] = (0.2 * main + g0[i] + K * near) / w0w[i + 1, HALO : HALO + wide, :]
+        out[i] = (0.2 * main + gm[own + i + 1, 8 + HALO : 8 + HALO + wide, :] + K * near) * i0[i]
 
     each(tall, up_0, 16)
 
@@ -697,7 +721,9 @@
 def plain_halo(mesh_shape, own, frames):
     n_gx = mesh_shape[0]
     tall = own[0].shape[0]
-    extent, tiles = frames[0][0], own[2].shape[1] // 128
+    extent, tiles = frames[1][0], own[2].shape[1] // 128
+    inverses = 1.0 / own[1]
+    own = (K * own[0] * inverses, *own[1:])
     parts = ()
     if n_gx > 1:
         odd = lax.axis_index("gx") % 2
@@ -709,7 +735,7 @@
     y_slabs = call(functools.partial(y_pack_kernel, mesh_shape), [slab, slab])(*own, *parts)
     y_parts = [ring(s, "gy", step) for s, step in zip(y_slabs, (1, -1))]
     fb, fw, matrix, z_a, z_b = call(functools.partial(z_pack_kernel, mesh_shape), frames)(*own, *parts, *y_parts)
-    return fb, fw, matrix, ring(z_a, "gz", 1), ring(z_b, "gz", -1)
+    return fb, fw, matrix, ring(z_a, "gz", 1), ring(z_b, "gz", -1), inverses
 
 
 def shared_halo(mesh_shape, own, frames):
@@ -719,8 +745,8 @@
     z_shape = (groups * per + strips, HALO, 128)
     y_shape = (2 * tall + tiles, HALO, 128)
     x_shape = (2 * per * tall + tiles, HALO, 128)
-    outs = [z_shape, z_shape, y_shape, y_shape, x_shape] + [a.shape for a in own]
-    z_tail, z_head, y_tail, y_head, x_own, *here = call(face_kernel, outs, fetch=True)(*own)
+    outs = [z_shape, z_shape, y_shape, y_shape, x_shape] + [a.shape for a in own] + [own[0].shape]
+    z_tail, z_head, y_tail, y_head, x_own, *here, inverses = call(face_kernel, outs, fetch=True)(*own)
 
     z_got = (ring(z_tail, "gz", 1), ring(z_head, "gz", -1))
     y_got = (ring(y_tail, "gy", 1), ring(y_head, "gy", -1))
@@ -733,9 +759,10 @@
     z_other = swap(z_both, "gx", 0)
     y_other = [swap(y, "gx", 0) for y in y_got]
     edge_other = [swap(y, "gx", 0) for y in edge_got]
-    return call(functools.partial(frame_kernel, mesh_shape), frames)(
+    made = call(functools.partial(frame_kernel, mesh_shape), frames)(
         *here, other, *z_got, z_other, *y_got, *y_other, *edge_got, *edge_other
     )
+    return *made, inverses
 
 
 def per_device(mesh_shape, sources, stiffness, coarse_inverse):
@@ -749,19 +776,18 @@
     source = sources[0]
     own = (source, stiffness, coarse_inverse)
     rows = wide + 2 * HALO
-    frame = (extent, rows, 128)
+    frame, padded = (extent, rows, 128), (extent + 2, rows + 16, 128)
     z_slab = (extent // HALO + (tiles + 1) // 2, rows, 128)
-    frames = [frame, frame, (9 * tiles, HALO, 128), z_slab, z_slab]
+    frames = [padded, frame, (9 * tiles, HALO, 128), z_slab, z_slab]
     exchange = shared_halo if n_gx == 2 else plain_halo
-    fb, fw, matrix, z_a, z_b = exchange(mesh_shape, own, frames)
-    padded = (extent + 2, rows + 16, 128)
+    gm, fw, matrix, z_a, z_b, inverses = exchange(mesh_shape, own, frames)
     half, half_rows = extent // 2, rows // 2
-    level1 = (half + 2, half_rows + 16, 128)
+    level1, plain1 = (half + 2, half_rows + 16, 128), (half, half_rows, 128)
     window, face = (tall + 2, rows, 128), (tall, wide, 128)
     message = (count, wide // 2, 128)
-    outs = [message, window, window, face, face, face] + [level1] * 6
-    scratch = [padded] * 4 + [frame] + [(half, rows, 128)] * 4 + [(2, tall // 4, wide // 2, 128)]
-    send, *state = call(functools.partial(down_kernel, mesh_shape), outs, scratch)(fb, fw, z_a, z_b)
+    outs = [message, padded, padded, padded, frame] + [level1] * 2 + [plain1] * 2 + [level1] * 2 + [plain1] * 2
+    scratch = [(half, rows, 128)] * 4 + [(2, tall // 4, wide // 2, 128)]
+    send, *state = call(functools.partial(down_kernel, mesh_shape), outs, scratch)(gm, fw, z_a, z_b)
     recv = lax.all_to_all(send, AXES, 0, 0, tiled=True)
     size_x, size_y, size_z = n_gx * tall // 4, n_gy * wide // 4, n_gz * deep // 4
     pad2 = (size_x + 2, size_y + 16, size_z)
@@ -769,13 +795,15 @@
     pad3 = (x3 + 2, rows3 + 16, size_z)
     n2, lane_tiles = extent // 4, size_z // 128
     scratch = [
-        pad2, (size_x, size_y, size_z), pad2, pad2, (size_x + 4, lane_tiles, size_y + 16, 128), (x3, lane_tiles, size_y, 128),
-        (lane_tiles, size_y, 128), (lane_tiles, size_y, 128), pad3, (x3, rows3, size_z), pad3, pad3,
+        pad2, *[(size_x, size_y, size_z)] * 2, pad2, pad2, (size_x + 4, lane_tiles, size_y + 16, 128), (x3, lane_tiles, size_y, 128),
+        (lane_tiles, size_y, 128), (lane_tiles, size_y, 128), pad3, *[(x3, rows3, size_z)] * 2, pad3, pad3,
         (x3 // 2 + 2, lane_tiles, rows3 + 16, 128),
-        (x3 // 2, rows3 // 2, size_z), (8, 128), level1, level1, (n2, 16, 128), (n2, 16, 128),
+        (x3 // 2, rows3 // 2, size_z), level1, level1, (n2, 16, 128), (n2, 16, 128),
         (half, rows, 128), (half, rows, 128), window, face,
     ]
-    (pressure,) = call(functools.partial(up_kernel, mesh_shape), [face], scratch, False)(recv, matrix, z_a, z_b, *state)
+    (pressure,) = call(functools.partial(up_kernel, mesh_shape), [face], scratch, False)(
+        recv, matrix, z_a, z_b, gm, fw, inverses, *state
+    )
     return pressure[None]
 
 

time: 46.4 us -> 45.5 us (0.981)
  Pallas kernels: 6.88 us -> 6 us
    pallas_call x5, Pallas kernels: 6.88 us -> 6 us  [call(): return lambda *values: run(*map(place, values))]
where the time goes in v1:
time: 45.5 us; the launch traced here: 45.4 us
  waiting for transfers between devices  16 us (35%)
  blocking collectives  12.9 us (28%)
  starting transfers between devices  10.5 us (23%)
  Pallas kernels  6 us (13%)
    ppermute x6, waiting for transfers between devices, ring(): lax.ppermute(values, axis, [(i, (i + step) % count) for i in range(count)])  15.1 us
    all_to_all x1, blocking collectives, per_device(): recv = lax.all_to_all(send, AXES, 0, 0, tiled=True)  12.9 us
    ppermute x6, starting transfers between devices, ring(): lax.ppermute(values, axis, [(i, (i + step) % count) for i in range(count)])  9.94 us
    pallas_call x5, Pallas kernels, call(): return lambda *values: run(*map(place, values))  6 us
  transfers between devices with their start and end apart: 12, of which 7 were waited for; matrix products, arithmetic and copies ran while one was open for 0% of the time, Pallas kernels for 0%

profile of v1, /device:TPU:0, one launch (start us, length us, event | category | flops | bytes accessed | tf_op | source)
XLA Modules:
  0.0 45.4 jit_solution(9164741797242395897)
XLA Ops:
  0.0 1.2 %shard_map.37 = (f32[5,8,128]{2,1,0:T(8,128)S(1)}, f32[5,8,128]{2,1,0:T(8,128)S(1)}, f32[34,8,128]{2,1,0:T(8,128)S(1)}, f32[34,8,128]{2,1,0:T(8,128)S(1)}, f32[6...) custom-call(f32[16,16,128]{2,1,0:T(8,128)} %bitcast.2, ...), custom_call_target="tpu_custom_call" | custom-call | tf_op jit(solution)/shard_map/pallas_call | solution.py:718
  1.2 3.0 %collective-permute-start.4 = (f32[34,8,128]{2,1,0:T(8,128)S(1)}, f32[34,8,128]{2,1,0:T(8,128)S(1)}, u32[]{:S(2)}, u32[]{:S(2)}) collective-permute-start(f32[34,8,128]{2,1,0:T(8,128)S(1)} %get-tuple-element.46), channel_id=1, source_target_pairs={{0,4},{4,8},{8,12},{12,0},{1,5},{5,9},{9,13},{13,1},{2,6},{6,10},{... | collective-permute-start | bytes 417800 | tf_op jit(solution)/shard_map/ppermute | solution.py:29
  4.2 1.0 %collective-permute-start.5 = (f32[34,8,128]{2,1,0:T(8,128)S(1)}, f32[34,8,128]{2,1,0:T(8,128)S(1)}, u32[]{:S(2)}, u32[]{:S(2)}) collective-permute-start(f32[34,8,128]{2,1,0:T(8,128)S(1)} %get-tuple-element.47), channel_id=1, source_target_pairs={{0,12},{4,0},{8,4},{12,8},{1,13},{5,1},{9,5},{13,9},{2,14},{6,2},{... | collective-permute-start | bytes 417800 | tf_op jit(solution)/shard_map/ppermute | solution.py:29
  5.2 0.0 collective-permute-start
  5.2 4.5 %collective-permute-done.4.refs_7_ = f32[34,8,128]{2,1,0:T(8,128)S(1)} collective-permute-done((f32[34,8,128]{2,1,0:T(8,128)S(1)}, f32[34,8,128]{2,1,0:T(8,128)S(1)}, u32[]{:S(2)}, u32[]{:S(2)}) %collective-permute-start.4) | collective-permute-done | bytes 139296 | tf_op jit(solution)/shard_map/ppermute | solution.py:29
  9.7 0.0 collective-permute-start.6
  9.7 2.4 %collective-permute-done.5.refs_8_ = f32[34,8,128]{2,1,0:T(8,128)S(1)} collective-permute-done((f32[34,8,128]{2,1,0:T(8,128)S(1)}, f32[34,8,128]{2,1,0:T(8,128)S(1)}, u32[]{:S(2)}, u32[]{:S(2)}) %collective-permute-start.5) | collective-permute-done | bytes 139296 | tf_op jit(solution)/shard_map/ppermute | solution.py:29
  12.1 0.0 collective-permute-start.7
  12.1 1.6 %collective-permute-start.1 = (f32[5,8,128]{2,1,0:T(8,128)S(1)}, f32[5,8,128]{2,1,0:T(8,128)S(1)}, u32[]{:S(2)}, u32[]{:S(2)}) collective-permute-start(f32[5,8,128]{2,1,0:T(8,128)S(1)} %get-tuple-element.41), channel_id=1, source_target_pairs={{0,1},{1,2},{2,3},{3,0},{4,5},{5,6},{6,7},{7,4},{8,9},{9,10},{10,1... | collective-permute-start | bytes 61448 | tf_op jit(solution)/shard_map/ppermute | solution.py:29
  13.7 2.2 %collective-permute-start.2 = (f32[5,8,128]{2,1,0:T(8,128)S(1)}, f32[5,8,128]{2,1,0:T(8,128)S(1)}, u32[]{:S(2)}, u32[]{:S(2)}) collective-permute-start(f32[5,8,128]{2,1,0:T(8,128)S(1)} %get-tuple-element.42), channel_id=1, source_target_pairs={{0,3},{1,0},{2,1},{3,2},{4,7},{5,4},{6,5},{7,6},{8,11},{9,8},{10,9... | collective-permute-start | bytes 61448 | tf_op jit(solution)/shard_map/ppermute | solution.py:29
  15.9 1.8 %collective-permute-done.1.refs_0_.refs_4_ = f32[5,8,128]{2,1,0:T(8,128)S(1)} collective-permute-done((f32[5,8,128]{2,1,0:T(8,128)S(1)}, f32[5,8,128]{2,1,0:T(8,128)S(1)}, u32[]{:S(2)}, u32[]{:S(2)}) %collective-permute-start.1) | collective-permute-done | bytes 20512 | tf_op jit(solution)/shard_map/ppermute | solution.py:29
  17.7 0.0 collective-permute-done.2.refs_1_.refs_5_
  17.7 1.5 %collective-permute-start.8 = (f32[6,8,128]{2,1,0:T(8,128)S(1)}, f32[6,8,128]{2,1,0:T(8,128)S(1)}, u32[]{:S(2)}, u32[]{:S(2)}) collective-permute-start(f32[6,8,128]{2,1,0:T(8,128)S(1)} %get-tuple-element.48), channel_id=1, source_target_pairs={{0,4},{4,8},{8,12},{12,0},{1,5},{5,9},{9,13},{13,1},{2,6},{6,10},{... | collective-permute-start | bytes 73736 | tf_op jit(solution)/shard_map/ppermute | solution.py:29
  19.2 0.0 collective-permute-start.3
  19.2 3.2 %collective-permute-done.8.refs_11_ = f32[6,8,128]{2,1,0:T(8,128)S(1)} collective-permute-done((f32[6,8,128]{2,1,0:T(8,128)S(1)}, f32[6,8,128]{2,1,0:T(8,128)S(1)}, u32[]{:S(2)}, u32[]{:S(2)}) %collective-permute-start.8) | collective-permute-done | bytes 24608 | tf_op jit(solution)/shard_map/ppermute | solution.py:29
  22.5 0.5 %collective-permute-start.9 = (f32[6,8,128]{2,1,0:T(8,128)S(1)}, f32[6,8,128]{2,1,0:T(8,128)S(1)}, u32[]{:S(2)}, u32[]{:S(2)}) collective-permute-start(f32[6,8,128]{2,1,0:T(8,128)S(1)} %get-tuple-element.49), channel_id=1, source_target_pairs={{0,12},{4,0},{8,4},{12,8},{1,13},{5,1},{9,5},{13,9},{2,14},{6,2},{... | collective-permute-start | bytes 73736 | tf_op jit(solution)/shard_map/ppermute | solution.py:29
  23.0 3.3 %collective-permute-done.9.refs_12_ = f32[6,8,128]{2,1,0:T(8,128)S(1)} collective-permute-done((f32[6,8,128]{2,1,0:T(8,128)S(1)}, f32[6,8,128]{2,1,0:T(8,128)S(1)}, u32[]{:S(2)}, u32[]{:S(2)}) %collective-permute-start.9) | collective-permute-done | bytes 24608 | tf_op jit(solution)/shard_map/ppermute | solution.py:29
  26.3 0.0 collective-permute-start.10
  26.3 0.0 collective-permute-done.3.refs_6_
  26.3 0.5 %collective-permute-start.11 = (f32[6,8,128]{2,1,0:T(8,128)S(1)}, f32[6,8,128]{2,1,0:T(8,128)S(1)}, u32[]{:S(2)}, u32[]{:S(2)}) collective-permute-start(f32[6,8,128]{2,1,0:T(8,128)S(1)} %collective-permute-done.9.refs_12_), channel_id=1, source_target_pairs={{0,16},{16,0},{1,17},{17,1},{2,18},{18,2},{3,19},{19,3},{4,20},{20... | collective-permute-start | bytes 73736 | tf_op jit(solution)/shard_map/ppermute | solution.py:24
  26.8 0.7 %collective-permute-done.10.refs_13_ = f32[6,8,128]{2,1,0:T(8,128)S(1)} collective-permute-done((f32[6,8,128]{2,1,0:T(8,128)S(1)}, f32[6,8,128]{2,1,0:T(8,128)S(1)}, u32[]{:S(2)}, u32[]{:S(2)}) %collective-permute-start.10) | collective-permute-done | bytes 24608 | tf_op jit(solution)/shard_map/ppermute | solution.py:24
  27.5 0.2 collective-permute-done.11.refs_14_
  27.7 0.0 collective-permute-done.refs_3_
  27.7 0.0 collective-permute-done.6.refs_9_
  27.7 0.0 collective-permute-done.7.refs_10_
  27.7 0.1 shard_map.39
  27.8 2.4 %shard_map.40 = (f32[32,8,128]{2,1,0:T(8,128)S(1)}, f32[26,48,128]{2,1,0:T(8,128)S(1)}, f32[26,48,128]{2,1,0:T(8,128)S(1)}, f32[26,48,128]{2,1,0:T(8,128)S(1)}, ...) custom-call(f32[26,48,128]{2,1,0:T(8,128)S(1)} %get-tuple-element.50, ...), custom_call_target="tpu_custom_call" | custom-call | tf_op jit(solution)/shard_map/pallas_call | solution.py:718
  30.2 12.9 %all_to_all.5.refs_0_ = f32[32,8,128]{2,1,0:T(8,128)S(1)} all-to-all(f32[32,8,128]{2,1,0:T(8,128)S(1)} %get-tuple-element.54), channel_id=1, replica_groups=mesh['gx'=2,'gy'=4,'gz'=4] {'gx','gy','gz'}, dimensions={0} | all-to-all | bytes 262144 | tf_op jit(solution)/shard_map/all_to_all | solution.py:791
  43.1 2.3 %shard_map.41 = f32[16,16,128]{2,1,0:T(8,128)} custom-call(f32[32,8,128]{2,1,0:T(8,128)S(1)} %all_to_all.5.refs_0_, f32[18,8,128]{2,1,0:T(8,128)S(1)} %get-tuple-element.55.refs_1_, f32[4,32,128]{2,1,0:T(8,128)S(1)} %get-tuple-element.52.refs_2_, f32[4,32,128]{2,1,0:T(8,128)S(1)} %get-tuple-element.53.refs_3_, ...), custom_call_target="tpu_custom_call" | custom-call | tf_op jit(solution)/shard_map/pallas_call | solution.py:718
  (1 shorter events, 0.0 us)
Async XLA Ops:
  1.2 8.5 %collective-permute-start.4 = (f32[34,8,128]{2,1,0:T(8,128)S(1)}, f32[34,8,128]{2,1,0:T(8,128)S(1)}, u32[]{:S(2)}, u32[]{:S(2)}) collective-permute-start(f32[34,8,128]{2,1,0:T(8,128)S(1)} %get-tuple-element.46), channel_id=1, source_target_pairs={{0,4},{4,8},{8,12},{12,0},{1,5},{5,9},{9,13},{13,1},{2,6},{6,10},{... | collective-permute-start | bytes 417800 | tf_op jit(solution)/shard_map/ppermute | solution.py:29
  4.2 7.9 %collective-permute-start.5 = (f32[34,8,128]{2,1,0:T(8,128)S(1)}, f32[34,8,128]{2,1,0:T(8,128)S(1)}, u32[]{:S(2)}, u32[]{:S(2)}) collective-permute-start(f32[34,8,128]{2,1,0:T(8,128)S(1)} %get-tuple-element.47), channel_id=1, source_target_pairs={{0,12},{4,0},{8,4},{12,8},{1,13},{5,1},{9,5},{13,9},{2,14},{6,2},{... | collective-permute-start | bytes 417800 | tf_op jit(solution)/shard_map/ppermute | solution.py:29
  5.2 22.4 %collective-permute-start = (f32[66,8,128]{2,1,0:T(8,128)S(1)}, f32[66,8,128]{2,1,0:T(8,128)S(1)}, u32[]{:S(2)}, u32[]{:S(2)}) collective-permute-start(f32[66,8,128]{2,1,0:T(8,128)S(1)} %get-tuple-element.40), channel_id=1, source_target_pairs={{0,16},{16,0},{1,17},{17,1},{2,18},{18,2},{3,19},{19,3},{4,20},{20... | collective-permute-start | bytes 811016 | tf_op jit(solution)/shard_map/ppermute | solution.py:24
  9.7 18.0 %collective-permute-start.6 = (f32[34,8,128]{2,1,0:T(8,128)S(1)}, f32[34,8,128]{2,1,0:T(8,128)S(1)}, u32[]{:S(2)}, u32[]{:S(2)}) collective-permute-start(f32[34,8,128]{2,1,0:T(8,128)S(1)} %collective-permute-done.4.refs_7_), channel_id=1, source_target_pairs={{0,16},{16,0},{1,17},{17,1},{2,18},{18,2},{3,19},{19,3},{4,20},{20... | collective-permute-start | bytes 417800 | tf_op jit(solution)/shard_map/ppermute | solution.py:24
  12.1 15.6 %collective-permute-start.7 = (f32[34,8,128]{2,1,0:T(8,128)S(1)}, f32[34,8,128]{2,1,0:T(8,128)S(1)}, u32[]{:S(2)}, u32[]{:S(2)}) collective-permute-start(f32[34,8,128]{2,1,0:T(8,128)S(1)} %collective-permute-done.5.refs_8_), channel_id=1, source_target_pairs={{0,16},{16,0},{1,17},{17,1},{2,18},{18,2},{3,19},{19,3},{4,20},{20... | collective-permute-start | bytes 417800 | tf_op jit(solution)/shard_map/ppermute | solution.py:24
  12.1 5.6 %collective-permute-start.1 = (f32[5,8,128]{2,1,0:T(8,128)S(1)}, f32[5,8,128]{2,1,0:T(8,128)S(1)}, u32[]{:S(2)}, u32[]{:S(2)}) collective-permute-start(f32[5,8,128]{2,1,0:T(8,128)S(1)} %get-tuple-element.41), channel_id=1, source_target_pairs={{0,1},{1,2},{2,3},{3,0},{4,5},{5,6},{6,7},{7,4},{8,9},{9,10},{10,1... | collective-permute-start | bytes 61448 | tf_op jit(solution)/shard_map/ppermute | solution.py:29
  13.7 4.0 %collective-permute-start.2 = (f32[5,8,128]{2,1,0:T(8,128)S(1)}, f32[5,8,128]{2,1,0:T(8,128)S(1)}, u32[]{:S(2)}, u32[]{:S(2)}) collective-permute-start(f32[5,8,128]{2,1,0:T(8,128)S(1)} %get-tuple-element.42), channel_id=1, source_target_pairs={{0,3},{1,0},{2,1},{3,2},{4,7},{5,4},{6,5},{7,6},{8,11},{9,8},{10,9... | collective-permute-start | bytes 61448 | tf_op jit(solution)/shard_map/ppermute | solution.py:29
  17.7 4.8 %collective-permute-start.8 = (f32[6,8,128]{2,1,0:T(8,128)S(1)}, f32[6,8,128]{2,1,0:T(8,128)S(1)}, u32[]{:S(2)}, u32[]{:S(2)}) collective-permute-start(f32[6,8,128]{2,1,0:T(8,128)S(1)} %get-tuple-element.48), channel_id=1, source_target_pairs={{0,4},{4,8},{8,12},{12,0},{1,5},{5,9},{9,13},{13,1},{2,6},{6,10},{... | collective-permute-start | bytes 73736 | tf_op jit(solution)/shard_map/ppermute | solution.py:29
  19.2 7.1 %collective-permute-start.3 = (f32[10,8,128]{2,1,0:T(8,128)S(1)}, f32[10,8,128]{2,1,0:T(8,128)S(1)}, u32[]{:S(2)}, u32[]{:S(2)}) collective-permute-start(f32[10,8,128]{2,1,0:T(8,128)S(1)} %get-tuple-element.45), channel_id=1, source_target_pairs={{0,16},{16,0},{1,17},{17,1},{2,18},{18,2},{3,19},{19,3},{4,20},{20... | collective-permute-start | bytes 122888 | tf_op jit(solution)/shard_map/ppermute | solution.py:24
  22.5 3.8 %collective-permute-start.9 = (f32[6,8,128]{2,1,0:T(8,128)S(1)}, f32[6,8,128]{2,1,0:T(8,128)S(1)}, u32[]{:S(2)}, u32[]{:S(2)}) collective-permute-start(f32[6,8,128]{2,1,0:T(8,128)S(1)} %get-tuple-element.49), channel_id=1, source_target_pairs={{0,12},{4,0},{8,4},{12,8},{1,13},{5,1},{9,5},{13,9},{2,14},{6,2},{... | collective-permute-start | bytes 73736 | tf_op jit(solution)/shard_map/ppermute | solution.py:29
  26.3 1.2 %collective-permute-start.10 = (f32[6,8,128]{2,1,0:T(8,128)S(1)}, f32[6,8,128]{2,1,0:T(8,128)S(1)}, u32[]{:S(2)}, u32[]{:S(2)}) collective-permute-start(f32[6,8,128]{2,1,0:T(8,128)S(1)} %collective-permute-done.8.refs_11_), channel_id=1, source_target_pairs={{0,16},{16,0},{1,17},{17,1},{2,18},{18,2},{3,19},{19,3},{4,20},{20... | collective-permute-start | bytes 73736 | tf_op jit(solution)/shard_map/ppermute | solution.py:24
  26.3 1.4 %collective-permute-start.11 = (f32[6,8,128]{2,1,0:T(8,128)S(1)}, f32[6,8,128]{2,1,0:T(8,128)S(1)}, u32[]{:S(2)}, u32[]{:S(2)}) collective-permute-start(f32[6,8,128]{2,1,0:T(8,128)S(1)} %collective-permute-done.9.refs_12_), channel_id=1, source_target_pairs={{0,16},{16,0},{1,17},{17,1},{2,18},{18,2},{3,19},{19,3},{4,20},{20... | collective-permute-start | bytes 73736 | tf_op jit(solution)/shard_map/ppermute | solution.py:24

commit v2 on v1

--- a/solution.py
+++ b/solution.py
@@ -438,17 +438,28 @@
             for ref, value in zip((tm, ts, um, us), totals):
                 ref[x2, row : row + 8, :] = value
 
-        def pairs(ref):
-            return lane_pairs(ref[x2, pl.ds(0, half_rows, stride=2), :] + ref[x2, pl.ds(1, half_rows, stride=2), :], 1)
-
-        for t_ref, u_ref, w_out, g_out, i_out in ((tm, um, w1m, g1m, i1m), (ts, us, w1s, g1s, i1s)):
-            weights = 0.0625 * pairs(u_ref)
-            inverses = inverse(weights)
-            w_out[x2, :, :] = weights
-            i_out[x2, :, :] = inverses
-            g_out[x2 + 1, 8 : 8 + half_rows, :] = (0.125 * K) * pairs(t_ref) * inverses
-
-    each(half, residual, 12)
+    each(half, residual, half)
+    src, dst = iota((128, 128), 0), iota((128, 128), 1)
+    pair = src // 2 == dst // 2
+
+    def coarsen(first):
+        rows_of = [
+            ref[first * 4 + i, pl.ds(0, half_rows, stride=2), :] + ref[first * 4 + i, pl.ds(1, half_rows, stride=2), :]
+            for i in range(4)
+            for ref in (tm, um, ts, us)
+        ]
+        sums = select_lanes(jnp.concatenate(rows_of, axis=0), pair)
+        for i in range(4):
+            x = first * 4 + i
+            for j, (w_out, g_out, i_out) in enumerate(((w1m, g1m, i1m), (w1s, g1s, i1s))):
+                at = (4 * i + 2 * j) * half_rows
+                weights = 0.0625 * sums[at + half_rows : at + 2 * half_rows]
+                inverses = inverse(weights)
+                w_out[x] = weights
+                i_out[x] = inverses
+                g_out[x + 1, 8 : 8 + half_rows, :] = (0.125 * K) * sums[at : at + half_rows] * inverses
+
+    each(half // 4, coarsen, 4)
 
     factors_1 = inside(half_rows, 2)
     each(half, lambda x: smooth((g1m, g1s), (v1m, v1s), factors_1, x, half_rows, 2), 16)

time: 45.5 us -> 45.1 us (level)
  Pallas kernels: 6 us -> 5.53 us
    pallas_call x5, Pallas kernels: 6 us -> 5.53 us  [call(): return lambda *values: run(*map(place, values))]
where the time goes in v2:
time: 45.1 us; the launch traced here: 44.9 us
  waiting for transfers between devices  16 us (35%)
  blocking collectives  12.9 us (29%)
  starting transfers between devices  10.5 us (23%)
  Pallas kernels  5.53 us (12%)
    ppermute x6, waiting for transfers between devices, ring(): lax.ppermute(values, axis, [(i, (i + step) % count) for i in range(count)])  15.1 us
    all_to_all x1, blocking collectives, per_device(): recv = lax.all_to_all(send, AXES, 0, 0, tiled=True)  12.9 us
    ppermute x6, starting transfers between devices, ring(): lax.ppermute(values, axis, [(i, (i + step) % count) for i in range(count)])  9.94 us
    pallas_call x5, Pallas kernels, call(): return lambda *values: run(*map(place, values))  5.53 us
  transfers between devices with their start and end apart: 12, of which 7 were waited for; matrix products, arithmetic and copies ran while one was open for 0% of the time, Pallas kernels for 0%

profile of v2, /device:TPU:0, one launch (start us, length us, event | category | flops | bytes accessed | tf_op | source)
XLA Modules:
  0.0 44.9 jit_solution(4868682088915448487)
XLA Ops:
  0.0 1.2 %shard_map.37 = (f32[5,8,128]{2,1,0:T(8,128)S(1)}, f32[5,8,128]{2,1,0:T(8,128)S(1)}, f32[34,8,128]{2,1,0:T(8,128)S(1)}, f32[34,8,128]{2,1,0:T(8,128)S(1)}, f32[6...) custom-call(f32[16,16,128]{2,1,0:T(8,128)} %bitcast.2, ...), custom_call_target="tpu_custom_call" | custom-call | tf_op jit(solution)/shard_map/pallas_call | solution.py:729
  1.2 3.0 %collective-permute-start.4 = (f32[34,8,128]{2,1,0:T(8,128)S(1)}, f32[34,8,128]{2,1,0:T(8,128)S(1)}, u32[]{:S(2)}, u32[]{:S(2)}) collective-permute-start(f32[34,8,128]{2,1,0:T(8,128)S(1)} %get-tuple-element.46), channel_id=1, source_target_pairs={{0,4},{4,8},{8,12},{12,0},{1,5},{5,9},{9,13},{13,1},{2,6},{6,10},{... | collective-permute-start | bytes 417800 | tf_op jit(solution)/shard_map/ppermute | solution.py:29
  4.2 1.0 %collective-permute-start.5 = (f32[34,8,128]{2,1,0:T(8,128)S(1)}, f32[34,8,128]{2,1,0:T(8,128)S(1)}, u32[]{:S(2)}, u32[]{:S(2)}) collective-permute-start(f32[34,8,128]{2,1,0:T(8,128)S(1)} %get-tuple-element.47), channel_id=1, source_target_pairs={{0,12},{4,0},{8,4},{12,8},{1,13},{5,1},{9,5},{13,9},{2,14},{6,2},{... | collective-permute-start | bytes 417800 | tf_op jit(solution)/shard_map/ppermute | solution.py:29
  5.2 0.0 collective-permute-start
  5.2 4.5 %collective-permute-done.4.refs_7_ = f32[34,8,128]{2,1,0:T(8,128)S(1)} collective-permute-done((f32[34,8,128]{2,1,0:T(8,128)S(1)}, f32[34,8,128]{2,1,0:T(8,128)S(1)}, u32[]{:S(2)}, u32[]{:S(2)}) %collective-permute-start.4) | collective-permute-done | bytes 139296 | tf_op jit(solution)/shard_map/ppermute | solution.py:29
  9.7 0.0 collective-permute-start.6
  9.7 2.4 %collective-permute-done.5.refs_8_ = f32[34,8,128]{2,1,0:T(8,128)S(1)} collective-permute-done((f32[34,8,128]{2,1,0:T(8,128)S(1)}, f32[34,8,128]{2,1,0:T(8,128)S(1)}, u32[]{:S(2)}, u32[]{:S(2)}) %collective-permute-start.5) | collective-permute-done | bytes 139296 | tf_op jit(solution)/shard_map/ppermute | solution.py:29
  12.1 0.0 collective-permute-start.7
  12.1 1.6 %collective-permute-start.1 = (f32[5,8,128]{2,1,0:T(8,128)S(1)}, f32[5,8,128]{2,1,0:T(8,128)S(1)}, u32[]{:S(2)}, u32[]{:S(2)}) collective-permute-start(f32[5,8,128]{2,1,0:T(8,128)S(1)} %get-tuple-element.41), channel_id=1, source_target_pairs={{0,1},{1,2},{2,3},{3,0},{4,5},{5,6},{6,7},{7,4},{8,9},{9,10},{10,1... | collective-permute-start | bytes 61448 | tf_op jit(solution)/shard_map/ppermute | solution.py:29
  13.7 2.2 %collective-permute-start.2 = (f32[5,8,128]{2,1,0:T(8,128)S(1)}, f32[5,8,128]{2,1,0:T(8,128)S(1)}, u32[]{:S(2)}, u32[]{:S(2)}) collective-permute-start(f32[5,8,128]{2,1,0:T(8,128)S(1)} %get-tuple-element.42), channel_id=1, source_target_pairs={{0,3},{1,0},{2,1},{3,2},{4,7},{5,4},{6,5},{7,6},{8,11},{9,8},{10,9... | collective-permute-start | bytes 61448 | tf_op jit(solution)/shard_map/ppermute | solution.py:29
  15.9 1.8 %collective-permute-done.1.refs_0_.refs_4_ = f32[5,8,128]{2,1,0:T(8,128)S(1)} collective-permute-done((f32[5,8,128]{2,1,0:T(8,128)S(1)}, f32[5,8,128]{2,1,0:T(8,128)S(1)}, u32[]{:S(2)}, u32[]{:S(2)}) %collective-permute-start.1) | collective-permute-done | bytes 20512 | tf_op jit(solution)/shard_map/ppermute | solution.py:29
  17.7 0.0 collective-permute-done.2.refs_1_.refs_5_
  17.7 1.5 %collective-permute-start.8 = (f32[6,8,128]{2,1,0:T(8,128)S(1)}, f32[6,8,128]{2,1,0:T(8,128)S(1)}, u32[]{:S(2)}, u32[]{:S(2)}) collective-permute-start(f32[6,8,128]{2,1,0:T(8,128)S(1)} %get-tuple-element.48), channel_id=1, source_target_pairs={{0,4},{4,8},{8,12},{12,0},{1,5},{5,9},{9,13},{13,1},{2,6},{6,10},{... | collective-permute-start | bytes 73736 | tf_op jit(solution)/shard_map/ppermute | solution.py:29
  19.2 0.0 collective-permute-start.3
  19.2 3.2 %collective-permute-done.8.refs_11_ = f32[6,8,128]{2,1,0:T(8,128)S(1)} collective-permute-done((f32[6,8,128]{2,1,0:T(8,128)S(1)}, f32[6,8,128]{2,1,0:T(8,128)S(1)}, u32[]{:S(2)}, u32[]{:S(2)}) %collective-permute-start.8) | collective-permute-done | bytes 24608 | tf_op jit(solution)/shard_map/ppermute | solution.py:29
  22.5 0.5 %collective-permute-start.9 = (f32[6,8,128]{2,1,0:T(8,128)S(1)}, f32[6,8,128]{2,1,0:T(8,128)S(1)}, u32[]{:S(2)}, u32[]{:S(2)}) collective-permute-start(f32[6,8,128]{2,1,0:T(8,128)S(1)} %get-tuple-element.49), channel_id=1, source_target_pairs={{0,12},{4,0},{8,4},{12,8},{1,13},{5,1},{9,5},{13,9},{2,14},{6,2},{... | collective-permute-start | bytes 73736 | tf_op jit(solution)/shard_map/ppermute | solution.py:29
  23.0 3.3 %collective-permute-done.9.refs_12_ = f32[6,8,128]{2,1,0:T(8,128)S(1)} collective-permute-done((f32[6,8,128]{2,1,0:T(8,128)S(1)}, f32[6,8,128]{2,1,0:T(8,128)S(1)}, u32[]{:S(2)}, u32[]{:S(2)}) %collective-permute-start.9) | collective-permute-done | bytes 24608 | tf_op jit(solution)/shard_map/ppermute | solution.py:29
  26.3 0.0 collective-permute-start.10
  26.3 0.0 collective-permute-done.3.refs_6_
  26.3 0.5 %collective-permute-start.11 = (f32[6,8,128]{2,1,0:T(8,128)S(1)}, f32[6,8,128]{2,1,0:T(8,128)S(1)}, u32[]{:S(2)}, u32[]{:S(2)}) collective-permute-start(f32[6,8,128]{2,1,0:T(8,128)S(1)} %collective-permute-done.9.refs_12_), channel_id=1, source_target_pairs={{0,16},{16,0},{1,17},{17,1},{2,18},{18,2},{3,19},{19,3},{4,20},{20... | collective-permute-start | bytes 73736 | tf_op jit(solution)/shard_map/ppermute | solution.py:24
  26.8 0.7 %collective-permute-done.10.refs_13_ = f32[6,8,128]{2,1,0:T(8,128)S(1)} collective-permute-done((f32[6,8,128]{2,1,0:T(8,128)S(1)}, f32[6,8,128]{2,1,0:T(8,128)S(1)}, u32[]{:S(2)}, u32[]{:S(2)}) %collective-permute-start.10) | collective-permute-done | bytes 24608 | tf_op jit(solution)/shard_map/ppermute | solution.py:24
  27.5 0.2 collective-permute-done.11.refs_14_
  27.7 0.0 collective-permute-done.refs_3_
  27.7 0.0 collective-permute-done.6.refs_9_
  27.7 0.0 collective-permute-done.7.refs_10_
  27.7 0.1 shard_map.39
  27.8 2.0 %shard_map.40 = (f32[32,8,128]{2,1,0:T(8,128)S(1)}, f32[26,48,128]{2,1,0:T(8,128)S(1)}, f32[26,48,128]{2,1,0:T(8,128)S(1)}, f32[26,48,128]{2,1,0:T(8,128)S(1)}, ...) custom-call(f32[26,48,128]{2,1,0:T(8,128)S(1)} %get-tuple-element.50, ...), custom_call_target="tpu_custom_call" | custom-call | tf_op jit(solution)/shard_map/pallas_call | solution.py:729
  29.8 12.9 %all_to_all.5.refs_0_ = f32[32,8,128]{2,1,0:T(8,128)S(1)} all-to-all(f32[32,8,128]{2,1,0:T(8,128)S(1)} %get-tuple-element.54), channel_id=1, replica_groups=mesh['gx'=2,'gy'=4,'gz'=4] {'gx','gy','gz'}, dimensions={0} | all-to-all | bytes 262144 | tf_op jit(solution)/shard_map/all_to_all | solution.py:802
  42.6 2.3 %shard_map.41 = f32[16,16,128]{2,1,0:T(8,128)} custom-call(f32[32,8,128]{2,1,0:T(8,128)S(1)} %all_to_all.5.refs_0_, f32[18,8,128]{2,1,0:T(8,128)S(1)} %get-tuple-element.55.refs_1_, f32[4,32,128]{2,1,0:T(8,128)S(1)} %get-tuple-element.52.refs_2_, f32[4,32,128]{2,1,0:T(8,128)S(1)} %get-tuple-element.53.refs_3_, ...), custom_call_target="tpu_custom_call" | custom-call | tf_op jit(solution)/shard_map/pallas_call | solution.py:729
  (1 shorter events, 0.0 us)
Async XLA Ops:
  1.2 8.5 %collective-permute-start.4 = (f32[34,8,128]{2,1,0:T(8,128)S(1)}, f32[34,8,128]{2,1,0:T(8,128)S(1)}, u32[]{:S(2)}, u32[]{:S(2)}) collective-permute-start(f32[34,8,128]{2,1,0:T(8,128)S(1)} %get-tuple-element.46), channel_id=1, source_target_pairs={{0,4},{4,8},{8,12},{12,0},{1,5},{5,9},{9,13},{13,1},{2,6},{6,10},{... | collective-permute-start | bytes 417800 | tf_op jit(solution)/shard_map/ppermute | solution.py:29
  4.2 7.9 %collective-permute-start.5 = (f32[34,8,128]{2,1,0:T(8,128)S(1)}, f32[34,8,128]{2,1,0:T(8,128)S(1)}, u32[]{:S(2)}, u32[]{:S(2)}) collective-permute-start(f32[34,8,128]{2,1,0:T(8,128)S(1)} %get-tuple-element.47), channel_id=1, source_target_pairs={{0,12},{4,0},{8,4},{12,8},{1,13},{5,1},{9,5},{13,9},{2,14},{6,2},{... | collective-permute-start | bytes 417800 | tf_op jit(solution)/shard_map/ppermute | solution.py:29
  5.2 22.4 %collective-permute-start = (f32[66,8,128]{2,1,0:T(8,128)S(1)}, f32[66,8,128]{2,1,0:T(8,128)S(1)}, u32[]{:S(2)}, u32[]{:S(2)}) collective-permute-start(f32[66,8,128]{2,1,0:T(8,128)S(1)} %get-tuple-element.40), channel_id=1, source_target_pairs={{0,16},{16,0},{1,17},{17,1},{2,18},{18,2},{3,19},{19,3},{4,20},{20... | collective-permute-start | bytes 811016 | tf_op jit(solution)/shard_map/ppermute | solution.py:24
  9.7 18.0 %collective-permute-start.6 = (f32[34,8,128]{2,1,0:T(8,128)S(1)}, f32[34,8,128]{2,1,0:T(8,128)S(1)}, u32[]{:S(2)}, u32[]{:S(2)}) collective-permute-start(f32[34,8,128]{2,1,0:T(8,128)S(1)} %collective-permute-done.4.refs_7_), channel_id=1, source_target_pairs={{0,16},{16,0},{1,17},{17,1},{2,18},{18,2},{3,19},{19,3},{4,20},{20... | collective-permute-start | bytes 417800 | tf_op jit(solution)/shard_map/ppermute | solution.py:24
  12.1 15.6 %collective-permute-start.7 = (f32[34,8,128]{2,1,0:T(8,128)S(1)}, f32[34,8,128]{2,1,0:T(8,128)S(1)}, u32[]{:S(2)}, u32[]{:S(2)}) collective-permute-start(f32[34,8,128]{2,1,0:T(8,128)S(1)} %collective-permute-done.5.refs_8_), channel_id=1, source_target_pairs={{0,16},{16,0},{1,17},{17,1},{2,18},{18,2},{3,19},{19,3},{4,20},{20... | collective-permute-start | bytes 417800 | tf_op jit(solution)/shard_map/ppermute | solution.py:24
  12.1 5.6 %collective-permute-start.1 = (f32[5,8,128]{2,1,0:T(8,128)S(1)}, f32[5,8,128]{2,1,0:T(8,128)S(1)}, u32[]{:S(2)}, u32[]{:S(2)}) collective-permute-start(f32[5,8,128]{2,1,0:T(8,128)S(1)} %get-tuple-element.41), channel_id=1, source_target_pairs={{0,1},{1,2},{2,3},{3,0},{4,5},{5,6},{6,7},{7,4},{8,9},{9,10},{10,1... | collective-permute-start | bytes 61448 | tf_op jit(solution)/shard_map/ppermute | solution.py:29
  13.7 4.0 %collective-permute-start.2 = (f32[5,8,128]{2,1,0:T(8,128)S(1)}, f32[5,8,128]{2,1,0:T(8,128)S(1)}, u32[]{:S(2)}, u32[]{:S(2)}) collective-permute-start(f32[5,8,128]{2,1,0:T(8,128)S(1)} %get-tuple-element.42), channel_id=1, source_target_pairs={{0,3},{1,0},{2,1},{3,2},{4,7},{5,4},{6,5},{7,6},{8,11},{9,8},{10,9... | collective-permute-start | bytes 61448 | tf_op jit(solution)/shard_map/ppermute | solution.py:29
  17.7 4.8 %collective-permute-start.8 = (f32[6,8,128]{2,1,0:T(8,128)S(1)}, f32[6,8,128]{2,1,0:T(8,128)S(1)}, u32[]{:S(2)}, u32[]{:S(2)}) collective-permute-start(f32[6,8,128]{2,1,0:T(8,128)S(1)} %get-tuple-element.48), channel_id=1, source_target_pairs={{0,4},{4,8},{8,12},{12,0},{1,5},{5,9},{9,13},{13,1},{2,6},{6,10},{... | collective-permute-start | bytes 73736 | tf_op jit(solution)/shard_map/ppermute | solution.py:29
  19.2 7.1 %collective-permute-start.3 = (f32[10,8,128]{2,1,0:T(8,128)S(1)}, f32[10,8,128]{2,1,0:T(8,128)S(1)}, u32[]{:S(2)}, u32[]{:S(2)}) collective-permute-start(f32[10,8,128]{2,1,0:T(8,128)S(1)} %get-tuple-element.45), channel_id=1, source_target_pairs={{0,16},{16,0},{1,17},{17,1},{2,18},{18,2},{3,19},{19,3},{4,20},{20... | collective-permute-start | bytes 122888 | tf_op jit(solution)/shard_map/ppermute | solution.py:24
  22.5 3.8 %collective-permute-start.9 = (f32[6,8,128]{2,1,0:T(8,128)S(1)}, f32[6,8,128]{2,1,0:T(8,128)S(1)}, u32[]{:S(2)}, u32[]{:S(2)}) collective-permute-start(f32[6,8,128]{2,1,0:T(8,128)S(1)} %get-tuple-element.49), channel_id=1, source_target_pairs={{0,12},{4,0},{8,4},{12,8},{1,13},{5,1},{9,5},{13,9},{2,14},{6,2},{... | collective-permute-start | bytes 73736 | tf_op jit(solution)/shard_map/ppermute | solution.py:29
  26.3 1.2 %collective-permute-start.10 = (f32[6,8,128]{2,1,0:T(8,128)S(1)}, f32[6,8,128]{2,1,0:T(8,128)S(1)}, u32[]{:S(2)}, u32[]{:S(2)}) collective-permute-start(f32[6,8,128]{2,1,0:T(8,128)S(1)} %collective-permute-done.8.refs_11_), channel_id=1, source_target_pairs={{0,16},{16,0},{1,17},{17,1},{2,18},{18,2},{3,19},{19,3},{4,20},{20... | collective-permute-start | bytes 73736 | tf_op jit(solution)/shard_map/ppermute | solution.py:24
  26.3 1.4 %collective-permute-start.11 = (f32[6,8,128]{2,1,0:T(8,128)S(1)}, f32[6,8,128]{2,1,0:T(8,128)S(1)}, u32[]{:S(2)}, u32[]{:S(2)}) collective-permute-start(f32[6,8,128]{2,1,0:T(8,128)S(1)} %collective-permute-done.9.refs_12_), channel_id=1, source_target_pairs={{0,16},{16,0},{1,17},{17,1},{2,18},{18,2},{3,19},{19,3},{4,20},{20... | collective-permute-start | bytes 73736 | tf_op jit(solution)/shard_map/ppermute | solution.py:24
